TPU v7x, 8 devices: a whole 2x2x1 slice. The times are simulated.
8 devices in a mesh: batch: 1 (over z), row: 2 (over y), col: 4 (over x, core).
Axes of the slice: x: 2, y: 2, z: 1, core: 2. Of those that a mesh axis runs over, the one named last changes fastest.
Arguments:
- data_mat: bfloat16 [65536, 7168], P(('batch', 'row', 'col'))
- start_block: float32 [7168, 256], P('batch')
Outputs:
- output 1: float32 [7168, 256], P('batch')
- output 2: float32 [256], P('batch')
All inputs are finite; a program needn't handle non-finite values.
Results may differ from a plain program's by a relative error of at most 0.001.
Values are sent between devices in bfloat16 or wider.
A program may use at most 1 GiB of HBM per device.

v0:
```python
import jax
import jax.numpy as jnp
from jax import lax
from jax.sharding import PartitionSpec as P

SWEEPS = 4
GROUP_AXES = ("row", "col")
ROW_CONTRACT = (((0,), (0,)), ((), ()))


def cholesky_qr2(z_rows):
    z_low = z_rows.astype(jnp.bfloat16)
    gram_one = lax.psum(lax.dot_general(z_low, z_low, ROW_CONTRACT, preferred_element_type=jnp.float32), GROUP_AXES)
    half_done = lax.linalg.triangular_solve(jnp.linalg.cholesky(gram_one), z_rows, left_side=False, lower=True, transpose_a=True)
    gram_two = lax.psum(lax.dot_general(half_done, half_done, ROW_CONTRACT, precision=lax.Precision.HIGHEST, preferred_element_type=jnp.float32), GROUP_AXES)
    return lax.linalg.triangular_solve(jnp.linalg.cholesky(gram_two), half_done, left_side=False, lower=True, transpose_a=True)


def solution(mesh):
    def device_sweeps(data_local, start_block):
        basis_low = start_block.astype(jnp.bfloat16)
        for sweep_idx in range(SWEEPS):
            projected = jnp.dot(data_local, basis_low, preferred_element_type=jnp.float32).astype(jnp.bfloat16)
            pulled_part = lax.dot_general(data_local, projected, ROW_CONTRACT, preferred_element_type=jnp.float32)
            pulled_rows = lax.psum_scatter(pulled_part, GROUP_AXES, scatter_dimension=0, tiled=True)
            q_rows = cholesky_qr2(pulled_rows)
            if sweep_idx < SWEEPS - 1:
                basis_low = lax.all_gather(q_rows.astype(jnp.bfloat16), GROUP_AXES, axis=0, tiled=True)
        q_basis = lax.all_gather(q_rows, GROUP_AXES, axis=0, tiled=True)
        final_proj = jnp.dot(data_local, q_basis.astype(jnp.bfloat16), preferred_element_type=jnp.float32)
        ritz_vals = lax.psum(jnp.sum(final_proj * final_proj, axis=0), GROUP_AXES)
        return q_basis, ritz_vals

    return jax.shard_map(device_sweeps, mesh=mesh, in_specs=(P(("batch", "row", "col"), None), P("batch", None)), out_specs=(P("batch", None), P("batch")), check_vma=False)
```

profile of v0, /device:TPU:0, one launch (start us, length us, event | category | flops | bytes accessed | tf_op | source)
XLA Modules:
  0.0 1706.9 jit_solution(10511011159597308674)
XLA Ops:
  7.2 45.4 %convolution_convert_fusion.3.clone.4 = bf16[8192,256]{1,0:T(8,128)(2,1)} fusion(bf16[8192,7168]{1,0:T(8,128)(2,1)} %param.5, f32[7168,256]{1,0:T(8,128)} %param.6), kind=kOutput, calls=%fused_computation.20.clone.clone.clone.1 | convolution fusion | flops 30068703232 | bytes 128974848 | tf_op jit(solution)/shard_map/dot_general | solution.py:23
  52.6 46.0 %convolution_bitcast_fusion.3 = f32[7168,256]{0,1:T(8,128)} fusion(bf16[8192,7168]{1,0:T(8,128)(2,1)} %param.5, bf16[8192,256]{1,0:T(8,128)(2,1)} %convolution_convert_fusion.3.clone.4), kind=kOutput, calls=%fused_computation.24 | convolution fusion | flops 30064771072 | bytes 128974848 | tf_op jit(solution)/shard_map/dot_general | solution.py:24
  98.7 60.8 %reduce-scatter.5.cloned.1.call-done = f32[896,256]{0,1:T(8,128)} async-done(((f32[7168,256]{0,1:T(8,128)}), f32[896,256]{0,1:T(8,128)}) %reduce-scatter.5.cloned.1.call-update) | async-done | bytes 917520 | tf_op jit(solution)/shard_map/reduce_scatter | solution.py:25
  162.2 43.4 %all-reduce.10.cloned.1.call-done = f32[256,256]{0,1:T(8,128)} async-done(((f32[256,256]{0,1:T(8,128)}), f32[256,256]{0,1:T(8,128)}) %all-reduce.10.cloned.1.call-update) | async-done | bytes 262160 | tf_op jit(solution)/shard_map/psum | solution.py:13
  207.7 11.7 cholesky.382
  219.5 9.8 custom-call.25
  229.8 11.7 cholesky.399
  243.6 4.3 while.16
  247.9 19.7 %custom-call.26 = f32[2,128,128]{1,2,0:T(8,128)S(1)} custom-call(f32[2,128,128]{2,1,0:T(8,128)S(1)} %get-tuple-element.54), custom_call_target="InvertDiagBlocksLowerTriangular" | custom-call | tf_op jit(solution)/shard_map/triangular_solve/custom-call.0 | solution.py:14
  273.2 42.0 %all-reduce.12.cloned.1.call-done = f32[256,256]{0,1:T(8,128)} async-done(((f32[256,256]{0,1:T(8,128)}), f32[256,256]{0,1:T(8,128)}) %all-reduce.12.cloned.1.call-update) | async-done | bytes 262160 | tf_op jit(solution)/shard_map/psum | solution.py:15
  317.3 11.7 cholesky.416
  329.7 9.8 custom-call.27
  340.0 11.7 cholesky.433
  353.9 4.3 while.17
  358.2 19.7 %custom-call.28 = f32[2,128,128]{1,2,0:T(8,128)S(1)} custom-call(f32[2,128,128]{2,1,0:T(8,128)S(1)} %get-tuple-element.55), custom_call_target="InvertDiagBlocksLowerTriangular" | custom-call | tf_op jit(solution)/shard_map/triangular_solve/custom-call.0 | solution.py:16
  380.4 27.9 %all-gather.5.cloned.1.call-done = bf16[7168,256]{0,1:T(8,128)(2,1)} async-done(((bf16[896,256]{0,1:T(8,128)(2,1)}), bf16[7168,256]{0,1:T(8,128)(2,1)}) %all-gather.5.cloned.1.call-update) | async-done | bytes 3670032 | tf_op jit(solution)/shard_map/all_gather | solution.py:28
  408.3 45.5 %convolution_convert_fusion.2.clone.2 = bf16[256,8192]{1,0:T(8,128)(2,1)} fusion(bf16[7168,256]{0,1:T(8,128)(2,1)} %all-gather.5.cloned.1.call-done, bf16[8192,7168]{1,0:T(8,128)(2,1)} %param.5), kind=kOutput, calls=%fused_computation.19.clone.clone.clone | convolution fusion | flops 30066868224 | bytes 125304832 | tf_op jit(solution)/shard_map/dot_general | solution.py:23
  453.8 47.3 %convolution_bitcast_fusion.2 = f32[7168,256]{0,1:T(8,128)} fusion(bf16[8192,7168]{1,0:T(8,128)(2,1)} %param.5, bf16[256,8192]{1,0:T(8,128)(2,1)} %convolution_convert_fusion.2.clone.2), kind=kOutput, calls=%fused_computation.23 | convolution fusion | flops 30064771072 | bytes 128974848 | tf_op jit(solution)/shard_map/dot_general | solution.py:24
  501.6 57.6 %reduce-scatter.7.cloned.1.call-done = f32[896,256]{0,1:T(8,128)} async-done(((f32[7168,256]{0,1:T(8,128)}), f32[896,256]{0,1:T(8,128)}) %reduce-scatter.7.cloned.1.call-update) | async-done | bytes 917520 | tf_op jit(solution)/shard_map/reduce_scatter | solution.py:25
  561.7 43.5 %all-reduce.14.cloned.1.call-done = f32[256,256]{0,1:T(8,128)} async-done(((f32[256,256]{0,1:T(8,128)}), f32[256,256]{0,1:T(8,128)}) %all-reduce.14.cloned.1.call-update) | async-done | bytes 262160 | tf_op jit(solution)/shard_map/psum | solution.py:13
  607.3 11.7 cholesky.450
  619.7 9.8 custom-call.29
  630.0 11.7 cholesky.467
  647.9 19.7 %custom-call.30 = f32[2,128,128]{1,2,0:T(8,128)S(1)} custom-call(f32[2,128,128]{2,1,0:T(8,128)S(1)} %get-tuple-element.56), custom_call_target="InvertDiagBlocksLowerTriangular" | custom-call | tf_op jit(solution)/shard_map/triangular_solve/custom-call.0 | solution.py:14
  673.1 42.0 %all-reduce.16.cloned.1.call-done = f32[256,256]{0,1:T(8,128)} async-done(((f32[256,256]{0,1:T(8,128)}), f32[256,256]{0,1:T(8,128)}) %all-reduce.16.cloned.1.call-update) | async-done | bytes 262160 | tf_op jit(solution)/shard_map/psum | solution.py:15
  717.2 11.7 cholesky.484
  729.6 9.8 custom-call.31
  739.9 11.7 cholesky.501
  753.7 4.5 while.19
  758.3 19.7 %custom-call.32 = f32[2,128,128]{1,2,0:T(8,128)S(1)} custom-call(f32[2,128,128]{2,1,0:T(8,128)S(1)} %get-tuple-element.57), custom_call_target="InvertDiagBlocksLowerTriangular" | custom-call | tf_op jit(solution)/shard_map/triangular_solve/custom-call.0 | solution.py:16
  780.6 27.9 %all-gather.7.cloned.1.call-done = bf16[7168,256]{0,1:T(8,128)(2,1)} async-done(((bf16[896,256]{0,1:T(8,128)(2,1)}), bf16[7168,256]{0,1:T(8,128)(2,1)}) %all-gather.7.cloned.1.call-update) | async-done | bytes 3670032 | tf_op jit(solution)/shard_map/all_gather | solution.py:28
  808.4 45.5 %convolution_convert_fusion.1.clone.2 = bf16[256,8192]{1,0:T(8,128)(2,1)} fusion(bf16[7168,256]{0,1:T(8,128)(2,1)} %all-gather.7.cloned.1.call-done, bf16[8192,7168]{1,0:T(8,128)(2,1)} %param.5), kind=kOutput, calls=%fused_computation.18.clone.clone.clone | convolution fusion | flops 30066868224 | bytes 125304832 | tf_op jit(solution)/shard_map/dot_general | solution.py:23
  853.9 47.3 %convolution_bitcast_fusion.1 = f32[7168,256]{0,1:T(8,128)} fusion(bf16[8192,7168]{1,0:T(8,128)(2,1)} %param.5, bf16[256,8192]{1,0:T(8,128)(2,1)} %convolution_convert_fusion.1.clone.2), kind=kOutput, calls=%fused_computation.22 | convolution fusion | flops 30064771072 | bytes 128974848 | tf_op jit(solution)/shard_map/dot_general | solution.py:24
  901.5 57.8 %reduce-scatter.9.cloned.1.call-done = f32[896,256]{0,1:T(8,128)} async-done(((f32[7168,256]{0,1:T(8,128)}), f32[896,256]{0,1:T(8,128)}) %reduce-scatter.9.cloned.1.call-update) | async-done | bytes 917520 | tf_op jit(solution)/shard_map/reduce_scatter | solution.py:25
  961.9 43.5 %all-reduce.18.cloned.1.call-done = f32[256,256]{0,1:T(8,128)} async-done(((f32[256,256]{0,1:T(8,128)}), f32[256,256]{0,1:T(8,128)}) %all-reduce.18.cloned.1.call-update) | async-done | bytes 262160 | tf_op jit(solution)/shard_map/psum | solution.py:13
  1007.4 11.7 cholesky.518
  1019.8 9.8 custom-call.33
  1030.1 11.7 cholesky.535
  1043.9 4.3 while.20
  1048.2 19.7 %custom-call.34 = f32[2,128,128]{1,2,0:T(8,128)S(1)} custom-call(f32[2,128,128]{2,1,0:T(8,128)S(1)} %get-tuple-element.58), custom_call_target="InvertDiagBlocksLowerTriangular" | custom-call | tf_op jit(solution)/shard_map/triangular_solve/custom-call.0 | solution.py:14
  1073.4 42.0 %all-reduce.20.cloned.1.call-done = f32[256,256]{0,1:T(8,128)} async-done(((f32[256,256]{0,1:T(8,128)}), f32[256,256]{0,1:T(8,128)}) %all-reduce.20.cloned.1.call-update) | async-done | bytes 262160 | tf_op jit(solution)/shard_map/psum | solution.py:15
  1117.5 11.7 cholesky.552
  1129.9 9.8 custom-call.35
  1140.2 11.7 cholesky.569
  1158.4 19.7 %custom-call.36 = f32[2,128,128]{1,2,0:T(8,128)S(1)} custom-call(f32[2,128,128]{2,1,0:T(8,128)S(1)} %get-tuple-element.59), custom_call_target="InvertDiagBlocksLowerTriangular" | custom-call | tf_op jit(solution)/shard_map/triangular_solve/custom-call.0 | solution.py:16
  1180.7 27.9 %all-gather.9.cloned.1.call-done = bf16[7168,256]{0,1:T(8,128)(2,1)} async-done(((bf16[896,256]{0,1:T(8,128)(2,1)}), bf16[7168,256]{0,1:T(8,128)(2,1)}) %all-gather.9.cloned.1.call-update) | async-done | bytes 3670032 | tf_op jit(solution)/shard_map/all_gather | solution.py:28
  1208.5 45.5 %convolution_convert_fusion.clone.4 = bf16[256,8192]{1,0:T(8,128)(2,1)} fusion(bf16[7168,256]{0,1:T(8,128)(2,1)} %all-gather.9.cloned.1.call-done, bf16[8192,7168]{1,0:T(8,128)(2,1)} %param.5), kind=kOutput, calls=%fused_computation.17.clone.clone.clone.1 | convolution fusion | flops 30066868224 | bytes 125304832 | tf_op jit(solution)/shard_map/dot_general | solution.py:23
  1254.0 47.3 %convolution_bitcast_fusion = f32[7168,256]{0,1:T(8,128)} fusion(bf16[8192,7168]{1,0:T(8,128)(2,1)} %param.5, bf16[256,8192]{1,0:T(8,128)(2,1)} %convolution_convert_fusion.clone.4), kind=kOutput, calls=%fused_computation.21 | convolution fusion | flops 30064771072 | bytes 128974848 | tf_op jit(solution)/shard_map/dot_general | solution.py:24
  1301.8 57.6 %reduce-scatter.11.cloned.1.call-done = f32[896,256]{0,1:T(8,128)} async-done(((f32[7168,256]{0,1:T(8,128)}), f32[896,256]{0,1:T(8,128)}) %reduce-scatter.11.cloned.1.call-update) | async-done | bytes 917520 | tf_op jit(solution)/shard_map/reduce_scatter | solution.py:25
  1362.0 43.5 %all-reduce.22.cloned.1.call-done = f32[256,256]{0,1:T(8,128)} async-done(((f32[256,256]{0,1:T(8,128)}), f32[256,256]{0,1:T(8,128)}) %all-reduce.22.cloned.1.call-update) | async-done | bytes 262160 | tf_op jit(solution)/shard_map/psum | solution.py:13
  1407.5 11.7 cholesky.586
  1419.9 9.8 custom-call.37
  1430.3 11.7 cholesky.603
  1448.1 19.7 %custom-call.38 = f32[2,128,128]{1,2,0:T(8,128)S(1)} custom-call(f32[2,128,128]{2,1,0:T(8,128)S(1)} %get-tuple-element.60), custom_call_target="InvertDiagBlocksLowerTriangular" | custom-call | tf_op jit(solution)/shard_map/triangular_solve/custom-call.0 | solution.py:14
  1473.3 42.0 %all-reduce.24.cloned.1.call-done = f32[256,256]{0,1:T(8,128)} async-done(((f32[256,256]{0,1:T(8,128)}), f32[256,256]{0,1:T(8,128)}) %all-reduce.24.cloned.1.call-update) | async-done | bytes 262160 | tf_op jit(solution)/shard_map/psum | solution.py:15
  1517.4 11.7 cholesky.620
  1529.8 9.8 custom-call.39
  1540.1 11.7 cholesky.637
  1554.0 4.3 while.23
  1558.3 19.7 %custom-call.40 = f32[2,128,128]{1,2,0:T(8,128)S(1)} custom-call(f32[2,128,128]{2,1,0:T(8,128)S(1)} %get-tuple-element.61), custom_call_target="InvertDiagBlocksLowerTriangular" | custom-call | tf_op jit(solution)/shard_map/triangular_solve/custom-call.0 | solution.py:16
  1580.7 43.3 %all-gather.11.cloned.1.call-done = f32[7168,256]{0,1:T(8,128)} async-done(((f32[896,256]{0,1:T(8,128)}), f32[7168,256]{0,1:T(8,128)}) %all-gather.11.cloned.1.call-update) | async-done | bytes 7340048 | tf_op jit(solution)/shard_map/all_gather | solution.py:29
  1624.1 45.4 %fusion.4 = f32[256]{0:T(256)S(1)} fusion(bf16[8192,7168]{1,0:T(8,128)(2,1)} %param.5, f32[7168,256]{0,1:T(8,128)} %all-gather.11.cloned.1.call-done), kind=kOutput, calls=%fused_computation.27 | convolution fusion | flops 30070800384 | bytes 124781568 | tf_op jit(solution)/shard_map/dot_general | solution.py:30
  1669.5 22.3 %psum.71 = f32[256]{0:T(256)} all-reduce(f32[256]{0:T(256)S(1)} %fusion.4), channel_id=1, replica_groups=mesh['batch'=1,'row'=2,'col'=4] {'row','col'}, use_global_device_ids=true, to_apply=%region_17.20 | all-reduce | flops 256 | bytes 2048 | tf_op jit(solution)/shard_map/psum | solution.py:31
  1691.7 8.4 copy.20
  (216 shorter events, 119.8 us)
Async XLA Ops:
  7.2 152.3 %reduce-scatter.5.cloned.1.call-start = ((), (), s32[]{:S(2)}) async-start(), calls=%async_computation.4 | async-start | bytes 8257536 | tf_op jit(solution)/shard_map/reduce_scatter | solution.py:25
  98.6 107.0 %all-reduce.10.cloned.1.call-start = ((), (), s32[]{:S(2)}) async-start(), calls=%async_computation.5 | async-start | bytes 524288 | tf_op jit(solution)/shard_map/psum | solution.py:13
  162.0 153.2 %all-reduce.12.cloned.1.call-start = ((), (), s32[]{:S(2)}) async-start(), calls=%async_computation.6 | async-start | bytes 524288 | tf_op jit(solution)/shard_map/psum | solution.py:15
  273.1 135.2 %all-gather.5.cloned.1.call-start = ((), (), s32[]{:S(2)}) async-start(), calls=%async_computation.7 | async-start | bytes 4128768 | tf_op jit(solution)/shard_map/all_gather | solution.py:28
  380.4 178.8 %reduce-scatter.7.cloned.1.call-start = ((), (), s32[]{:S(2)}) async-start(), calls=%async_computation.8 | async-start | bytes 8257536 | tf_op jit(solution)/shard_map/reduce_scatter | solution.py:25
  501.2 104.1 %all-reduce.14.cloned.1.call-start = ((), (), s32[]{:S(2)}) async-start(), calls=%async_computation.9 | async-start | bytes 524288 | tf_op jit(solution)/shard_map/psum | solution.py:13
  561.7 153.4 %all-reduce.16.cloned.1.call-start = ((), (), s32[]{:S(2)}) async-start(), calls=%async_computation.10 | async-start | bytes 524288 | tf_op jit(solution)/shard_map/psum | solution.py:15
  673.0 135.4 %all-gather.7.cloned.1.call-start = ((), (), s32[]{:S(2)}) async-start(), calls=%async_computation.11 | async-start | bytes 4128768 | tf_op jit(solution)/shard_map/all_gather | solution.py:28
  780.5 178.8 %reduce-scatter.9.cloned.1.call-start = ((), (), s32[]{:S(2)}) async-start(), calls=%async_computation.12 | async-start | bytes 8257536 | tf_op jit(solution)/shard_map/reduce_scatter | solution.py:25
  901.3 104.1 %all-reduce.18.cloned.1.call-start = ((), (), s32[]{:S(2)}) async-start(), calls=%async_computation.13 | async-start | bytes 524288 | tf_op jit(solution)/shard_map/psum | solution.py:13
  961.8 153.6 %all-reduce.20.cloned.1.call-start = ((), (), s32[]{:S(2)}) async-start(), calls=%async_computation.14 | async-start | bytes 524288 | tf_op jit(solution)/shard_map/psum | solution.py:15
  1073.4 135.2 %all-gather.9.cloned.1.call-start = ((), (), s32[]{:S(2)}) async-start(), calls=%async_computation.15 | async-start | bytes 4128768 | tf_op jit(solution)/shard_map/all_gather | solution.py:28
  1180.6 178.8 %reduce-scatter.11.cloned.1.call-start = ((), (), s32[]{:S(2)}) async-start(), calls=%async_computation.16 | async-start | bytes 8257536 | tf_op jit(solution)/shard_map/reduce_scatter | solution.py:25
  1301.4 104.1 %all-reduce.22.cloned.1.call-start = ((), (), s32[]{:S(2)}) async-start(), calls=%async_computation.17 | async-start | bytes 524288 | tf_op jit(solution)/shard_map/psum | solution.py:13
  1361.9 153.4 %all-reduce.24.cloned.1.call-start = ((), (), s32[]{:S(2)}) async-start(), calls=%async_computation.18 | async-start | bytes 524288 | tf_op jit(solution)/shard_map/psum | solution.py:15
  1473.3 150.8 %all-gather.11.cloned.1.call-start = ((), (), s32[]{:S(2)}) async-start(), calls=%async_computation.19 | async-start | bytes 8257536 | tf_op jit(solution)/shard_map/all_gather | solution.py:29
Sparse Core Ops, SparseCore 0:
  98.7 60.6 reduce-scatter.4
  163.0 42.5 all-reduce.9
  273.3 41.8 all-reduce.11
  380.5 27.7 all-gather.4
  501.3 57.8 reduce-scatter.6
  562.6 42.5 all-reduce.13
  673.2 41.8 all-reduce.15
  780.6 27.7 all-gather.6
  901.4 57.8 reduce-scatter.8
  962.7 42.5 all-reduce.17
  1073.5 41.8 all-reduce.19
  1180.7 27.7 all-gather.8
  1301.5 57.8 reduce-scatter.10
  1362.9 42.5 all-reduce.21
  1473.4 41.8 all-reduce.23
  1580.9 43.1 all-gather.10
where the time goes:
time: 1710 us
  waiting for transfers between devices  703 us (41%)
  matrix products  458 us (27%)
  other arithmetic  445 us (26%)
  local copies, waits for them, and re-layouts  49 us (3%)
  between operations  25.4 us (1%)
  blocking collectives  22.3 us (1%)
    reduce_scatter x4, waiting for transfers between devices, device_sweeps(): lax.psum_scatter(pulled_part, GROUP_AXES, scatter_dimension=0, tiled=True)  234 us
    dot_general x4, matrix products, device_sweeps(): lax.dot_general(data_local, projected, ROW_CONTRACT, preferred_element_ty...  188 us
    dot_general x4, matrix products, device_sweeps(): jnp.dot(data_local, basis_low, preferred_element_type=jnp.float32)  182 us
    psum x4, waiting for transfers between devices, cholesky_qr2(): lax.psum(lax.dot_general(z_low, z_low, ROW_CONTRACT, preferred_element_ty...  174 us
    psum x4, waiting for transfers between devices, cholesky_qr2(): lax.psum(lax.dot_general(half_done, half_done, ROW_CONTRACT, precision=la...  168 us
    another operation x28, other arithmetic, cholesky_qr2(): jnp.linalg.cholesky(gram_two)  139 us
    another operation x27, other arithmetic, cholesky_qr2(): jnp.linalg.cholesky(gram_one)  138 us
    all_gather x3, waiting for transfers between devices, device_sweeps(): lax.all_gather(q_rows.astype(jnp.bfloat16), GROUP_AXES, axis=0, tiled=True)  83.6 us
  transfers between devices with their start and end apart: 16, of which 16 were waited for; matrix products, arithmetic and copies ran while one was open for 0% of the time, Pallas kernels for 0%

commit v1 on v0

v1 whole, which is shorter than its diff:
```python
import jax
import jax.numpy as jnp
from jax import lax
from jax.experimental import pallas as pl
from jax.experimental.pallas import tpu as pltpu
from jax.sharding import PartitionSpec as P

SWEEPS = 4
GROUP_AXES = ("row", "col")
ROW_CONTRACT = (((0,), (0,)), ((), ()))
LANE_CONTRACT = (((1,), (1,)), ((), ()))
PLAIN = (((1,), (0,)), ((), ()))
MESH = pl.DeviceIdType.MESH
HALF = 128
PEERS = 7
VMEM_BYTES = 60 * 1024 * 1024


def exact_dot(left, right, dims):
    return lax.dot_general(left, right, dims, precision=lax.Precision.HIGHEST, preferred_element_type=jnp.float32)


def invert_factor(block):
    lane = lax.broadcasted_iota(jnp.int32, (8, HALF), 1)
    sub = lax.broadcasted_iota(jnp.int32, (8, HALF), 0)
    for step in range(HALF // 8):
        base = 8 * step
        inside = (lane >= base) & (lane < base + 8)
        pivots = block[base:base + 8, :]
        cols = [jnp.broadcast_to(pivots[:, base + p:base + p + 1], (8, HALF)) for p in range(8)]
        low = jnp.where(inside, jnp.where(lane - base == sub, 1.0, 0.0), pivots)
        full = low
        scale = jnp.zeros((8, HALF), jnp.float32)
        inverse = jnp.zeros((8, HALF), jnp.float32)
        for p in range(8):
            root = lax.rsqrt(jnp.broadcast_to(cols[p][p:p + 1, :], (8, HALF)))
            recip = root * root
            here = sub == p
            scale = jnp.where(here, root, scale)
            inverse = jnp.where(here, recip, inverse)
            mult = jnp.where(here, 0.0, cols[p] * recip)
            for q in range(p + 1, 8):
                cols[q] = cols[q] - mult * jnp.broadcast_to(cols[q][p:p + 1, :], (8, HALF))
            full_row = jnp.broadcast_to(full[p:p + 1, :], (8, HALF))
            low_row = jnp.broadcast_to(low[p:p + 1, :], (8, HALF))
            full = full - mult * full_row
            low = low - jnp.where(sub > p, mult, 0.0) * low_row
        block[base:base + 8, :] = low * scale
        full = full * inverse
        rows = [jnp.broadcast_to(full[p:p + 1, :], (8, HALF)) for p in range(8)]
        for i in range(step + 1, HALF // 8):
            held = block[8 * i:8 * i + 8, :]
            acc = jnp.where(inside, 0.0, held)
            for p in range(8):
                acc = acc - jnp.broadcast_to(held[:, base + p:base + p + 1], (8, HALF)) * rows[p]
            block[8 * i:8 * i + 8, :] = acc


def factor_inverse(gram, work, inv_low):
    tri = lax.broadcasted_iota(jnp.int32, (HALF, HALF), 0) >= lax.broadcasted_iota(jnp.int32, (HALF, HALF), 1)
    inv_low[:HALF, HALF:] = jnp.zeros((HALF, HALF), jnp.float32)

    @pl.loop(0, 2)
    def _(half):
        @pl.when(half == 0)
        def _():
            work[...] = gram[0:HALF, :]

        @pl.when(half == 1)
        def _():
            upper = exact_dot(inv_low[:HALF, :HALF], gram[HALF:2 * HALF, :], PLAIN)
            work[...] = gram[2 * HALF:3 * HALF, :] - exact_dot(upper, upper, ROW_CONTRACT)
            inv_low[HALF:, :HALF] = exact_dot(upper, inv_low[:HALF, :HALF], ROW_CONTRACT)

        invert_factor(work)
        block_inv = jnp.where(tri, work[...], 0.0)

        @pl.when(half == 0)
        def _():
            inv_low[:HALF, :HALF] = block_inv

        @pl.when(half == 1)
        def _():
            inv_low[HALF:, HALF:] = block_inv
            inv_low[HALF:, :HALF] = -exact_dot(block_inv, inv_low[HALF:, :HALF], PLAIN)


def qr_kernel(z_ref, q_ref, all_ref, part, slots, gram, work, inv_low, sum_send, sum_recv, out_send, out_recv, cast_send, cast_recv):
    row, col = lax.axis_index("row"), lax.axis_index("col")
    me = row * 4 + col
    chunk = 3 * HALF // 8
    rows = z_ref.shape[0]

    def peer(offset):
        other = lax.rem(me + offset, 8)
        return (0, other // 4, lax.rem(other, 4)), other

    barrier = pltpu.get_barrier_semaphore()
    for offset in range(1, 8):
        pl.semaphore_signal(barrier, inc=1, device_id=peer(offset)[0], device_id_type=MESH)
    pl.semaphore_wait(barrier, PEERS)

    def share_gram(turn):
        mine = pl.ds(pl.multiple_of(me * chunk, 8), chunk)
        copies = []
        for offset in range(1, 8):
            device, other = peer(offset)
            copy = pltpu.make_async_remote_copy(
                src_ref=part.at[turn, pl.ds(pl.multiple_of(other * chunk, 8), chunk)],
                dst_ref=slots.at[turn, offset - 1],
                send_sem=sum_send.at[turn, offset - 1],
                recv_sem=sum_recv.at[turn, offset - 1],
                device_id=device,
                device_id_type=MESH,
            )
            copy.start()
            copies.append(copy)
        total = part[turn, mine, :]
        for offset in range(1, 8):
            copies[offset - 1].wait_recv()
            total = total + slots[turn, offset - 1]
        gram[turn, mine, :] = total
        spread = []
        for offset in range(1, 8):
            copy = pltpu.make_async_remote_copy(
                src_ref=gram.at[turn, mine],
                dst_ref=gram.at[turn, mine],
                send_sem=out_send.at[turn, offset - 1],
                recv_sem=out_recv.at[turn, offset - 1],
                device_id=peer(offset)[0],
                device_id_type=MESH,
            )
            copy.start()
            spread.append(copy)
        for copy in copies:
            copy.wait_send()
        for copy in spread:
            copy.wait()

    z_left, z_right = z_ref[:, :HALF].astype(jnp.bfloat16), z_ref[:, HALF:].astype(jnp.bfloat16)
    for place, (left, right) in enumerate(((z_left, z_left), (z_left, z_right), (z_right, z_right))):
        part[0, HALF * place:HALF * (place + 1), :] = lax.dot_general(left, right, ROW_CONTRACT, preferred_element_type=jnp.float32)

    q_ref[...] = z_ref[...]

    def turn_body(turn):
        share_gram(turn)
        factor_inverse(gram.at[turn], work, inv_low)

        @pl.loop(0, rows // HALF)
        def _(i):
            block = pl.ds(pl.multiple_of(i * HALF, HALF), HALF)
            q_ref[block, :] = exact_dot(q_ref[block, :], inv_low[...], LANE_CONTRACT)

        @pl.when(turn == 0)
        def _():
            for place, (left, right) in enumerate(((0, 0), (0, HALF), (HALF, HALF))):
                part[1, HALF * place:HALF * (place + 1), :] = exact_dot(q_ref[:, left:left + HALF], q_ref[:, right:right + HALF], ROW_CONTRACT)

    pl.loop(0, 2)(turn_body)

    core, x = lax.rem(col, 2), col // 2
    twin, x_side, y_side = (0, row, col + 1 - 2 * core), (0, row, core + 2 * (1 - x)), (0, 1 - row, col)
    x_index, y_index, far_index = row * 4 + x_side[2], (1 - row) * 4 + col, (1 - row) * 4 + x_side[2]
    upper, lower = pl.ds(0, rows // 2), pl.ds(rows // 2, rows // 2)
    whole = pl.ds(0, rows)
    all_ref[me] = q_ref[...].astype(jnp.bfloat16)

    def hand(slot, owner, piece, device):
        copy = pltpu.make_async_remote_copy(
            src_ref=all_ref.at[owner, piece],
            dst_ref=all_ref.at[owner, piece],
            send_sem=cast_send.at[slot],
            recv_sem=cast_recv.at[slot],
            device_id=device,
            device_id_type=MESH,
        )
        copy.start()
        return copy

    from_x = hand(0, me, whole, x_side)
    from_y = hand(1, me, whole, y_side)
    from_twin = hand(2, me, whole, twin)
    from_x.wait_recv()
    far_y = hand(3, x_index, upper, y_side)
    twin_x = hand(4, x_index, whole, twin)
    from_y.wait_recv()
    far_x = hand(5, y_index, lower, x_side)
    twin_y = hand(6, y_index, whole, twin)
    far_y.wait_recv()
    far_x.wait_recv()
    twin_far = hand(7, far_index, whole, twin)
    for copy in (from_twin, twin_x, twin_y, twin_far):
        copy.wait_recv()
    for copy in (from_x, from_y, from_twin, far_y, far_x, twin_x, twin_y, twin_far):
        copy.wait_send()


def orthonormalize(z_rows):
    rows, width = z_rows.shape
    return pl.pallas_call(
        qr_kernel,
        out_shape=(jax.ShapeDtypeStruct((rows, width), jnp.float32), jax.ShapeDtypeStruct((8, rows, width), jnp.bfloat16)),
        in_specs=[pl.BlockSpec(memory_space=pltpu.VMEM)],
        out_specs=(pl.BlockSpec(memory_space=pltpu.VMEM), pl.BlockSpec(memory_space=pltpu.VMEM)),
        scratch_shapes=[
            pltpu.VMEM((2, 3 * HALF, HALF), jnp.float32),
            pltpu.VMEM((2, PEERS, 3 * HALF // 8, HALF), jnp.float32),
            pltpu.VMEM((2, 3 * HALF, HALF), jnp.float32),
            pltpu.VMEM((HALF, HALF), jnp.float32),
            pltpu.VMEM((2 * HALF, 2 * HALF), jnp.float32),
            pltpu.SemaphoreType.DMA((2, PEERS)),
            pltpu.SemaphoreType.DMA((2, PEERS)),
            pltpu.SemaphoreType.DMA((2, PEERS)),
            pltpu.SemaphoreType.DMA((2, PEERS)),
            pltpu.SemaphoreType.DMA((8,)),
            pltpu.SemaphoreType.DMA((8,)),
        ],
        compiler_params=pltpu.CompilerParams(collective_id=0, has_side_effects=True),
        cost_estimate=pl.CostEstimate(flops=4 * 10**9, bytes_accessed=6 * 10**6, transcendentals=0),
        name="orthonormalize",
    )(z_rows)


def solution(mesh):
    def device_sweeps(data_local, start_block):
        basis_low = start_block.astype(jnp.bfloat16)
        for _ in range(SWEEPS):
            projected = jnp.dot(data_local, basis_low, preferred_element_type=jnp.float32).astype(jnp.bfloat16)
            pulled_part = lax.dot_general(data_local, projected, ROW_CONTRACT, preferred_element_type=jnp.float32)
            pulled_rows = lax.psum_scatter(pulled_part, GROUP_AXES, scatter_dimension=0, tiled=True)
            q_rows, basis_blocks = orthonormalize(pulled_rows)
            basis_low = basis_blocks.reshape(start_block.shape)
        q_basis = lax.all_gather(q_rows, GROUP_AXES, axis=0, tiled=True)
        final_proj = jnp.dot(data_local, basis_low, preferred_element_type=jnp.float32)
        ritz_vals = lax.psum(jnp.sum(final_proj * final_proj, axis=0), GROUP_AXES)
        return q_basis, ritz_vals

    return jax.shard_map(device_sweeps, mesh=mesh, in_specs=(P(("batch", "row", "col"), None), P("batch", None)), out_specs=(P("batch", None), P("batch")), check_vma=False)
```

time: 1710 us -> 1020 us (0.60)
  waiting for transfers between devices: 703 us -> 235 us
  other arithmetic: 445 us -> 0 us
  Pallas kernels: 0 us -> 276 us
  local copies, waits for them, and re-layouts: 49 us -> 6.6 us
    another operation x73 -> x0, other arithmetic: 435 us -> none  [the longest x28 139 us: cholesky_qr2(): jnp.linalg.cholesky(gram_two)]
    psum x8 -> x0, waiting for transfers between devices: 342 us -> none  [the longest x4 174 us: cholesky_qr2(): lax.psum(lax.dot_general(z_low, z_low, ROW_CONTRACT, preferred_element_ty...]
    pallas_call x0 -> x4, Pallas kernels: none -> 276 us  [orthonormalize(): pl.pallas_call(qr_kernel, out_shape=(jax.ShapeDtypeStruct((rows, width),...]
    all_gather x3 -> x0, waiting for transfers between devices: 83.6 us -> none  [device_sweeps(): lax.all_gather(q_rows.astype(jnp.bfloat16), GROUP_AXES, axis=0, tiled=True)]
    dot_general x9 -> x0, matrix products: 62.3 us -> none  [the longest x1 45.4 us: device_sweeps(): jnp.dot(data_local, q_basis.astype(jnp.bfloat16), preferred_element_type=...]
    dot_general x4, matrix products: 188 us -> 233 us  [device_sweeps(): lax.dot_general(data_local, projected, ROW_CONTRACT, preferred_element_ty...]
    dot_general x4 -> x5, matrix products: 182 us -> 227 us  [device_sweeps(): jnp.dot(data_local, basis_low, preferred_element_type=jnp.float32)]
    all_gather x1, waiting for transfers between devices: 43.3 us -> 0.01 us  [device_sweeps(): q_basis = lax.all_gather(q_rows, GROUP_AXES, axis=0, tiled=True)]
  transfers between devices with their start and end apart: 16 -> 5, of which waited for: 16 -> 4; matrix products, arithmetic and copies ran while one was open for 0% -> 4% of each run, Pallas kernels for 0% -> 0%
where the time goes in v1:
time: 1020 us; the launch traced here: 1010 us
  matrix products  460 us (45%)
  Pallas kernels  276 us (27%)
  waiting for transfers between devices  235 us (23%)
  blocking collectives  22.2 us (2%)
  between operations  14.3 us (1%)
    pallas_call x4, Pallas kernels, orthonormalize(): pl.pallas_call(qr_kernel, out_shape=(jax.ShapeDtypeStruct((rows, width),...  276 us
    reduce_scatter x4, waiting for transfers between devices, device_sweeps(): lax.psum_scatter(pulled_part, GROUP_AXES, scatter_dimension=0, tiled=True)  235 us
    dot_general x4, matrix products, device_sweeps(): lax.dot_general(data_local, projected, ROW_CONTRACT, preferred_element_ty...  233 us
    dot_general x5, matrix products, device_sweeps(): jnp.dot(data_local, basis_low, preferred_element_type=jnp.float32)  227 us
    psum x1, blocking collectives, device_sweeps(): ritz_vals = lax.psum(jnp.sum(final_proj * final_proj, axis=0), GROUP_AXES)  22.2 us
  transfers between devices with their start and end apart: 5, of which 4 were waited for; matrix products, arithmetic and copies ran while one was open for 4% of the time, Pallas kernels for 0%

profile of v1, /device:TPU:0, one launch (start us, length us, event | category | flops | bytes accessed | tf_op | source)
XLA Modules:
  0.0 1014.8 jit_solution(14361845645559741687)
XLA Ops:
  7.2 0.0 reduce-scatter.5.cloned.1.call-start
  7.2 45.4 %convolution_convert_fusion.3.clone.4 = bf16[8192,256]{1,0:T(8,128)(2,1)} fusion(bf16[8192,7168]{1,0:T(8,128)(2,1)} %param.2, f32[7168,256]{1,0:T(8,128)} %param.3), kind=kOutput, calls=%fused_computation.4.clone.clone.clone.1 | convolution fusion | flops 30068703232 | bytes 128974848 | tf_op jit(solution)/shard_map/dot_general | solution.py:229
  52.6 60.4 %convolution_bitcast_fusion.3 = f32[7168,256]{1,0:T(8,128)} fusion(bf16[8192,7168]{1,0:T(8,128)(2,1)} %param.2, bf16[8192,256]{1,0:T(8,128)(2,1)} %convolution_convert_fusion.3.clone.4), kind=kOutput, calls=%fused_computation.8 | convolution fusion | flops 30064771072 | bytes 128974848 | tf_op jit(solution)/shard_map/dot_general | solution.py:230
  113.1 0.0 reduce-scatter.5.cloned.1.call-update
  113.1 0.3 reduce-scatter.7.cloned.1.call-start
  113.3 60.6 %reduce-scatter.5.cloned.1.call-done.z_ref = f32[896,256]{1,0:T(8,128)} async-done(((f32[7168,256]{1,0:T(8,128)}), f32[896,256]{1,0:T(8,128)}) %reduce-scatter.5.cloned.1.call-update) | async-done | bytes 917520 | tf_op jit(solution)/shard_map/reduce_scatter | solution.py:231
  173.9 68.9 %orthonormalize.4 = (f32[896,256]{1,0:T(8,128)}, bf16[8,896,256]{2,1,0:T(8,128)(2,1)}) custom-call(f32[896,256]{1,0:T(8,128)} %reduce-scatter.5.cloned.1.call-done.z_ref), custom_call_target="tpu_custom_call" | custom-call | flops 4000000000 | bytes 6000000 | tf_op jit(solution)/shard_map/orthonormalize/pallas_call | solution.py:201
  242.8 45.7 %convolution_convert_fusion.2.clone.2 = bf16[256,8192]{1,0:T(8,128)(2,1)} fusion(bf16[7168,256]{1,0:T(8,128)(2,1)} %bitcast.47, bf16[8192,7168]{1,0:T(8,128)(2,1)} %param.2), kind=kOutput, calls=%fused_computation.3.clone.clone.clone | convolution fusion | flops 30066868224 | bytes 125304832 | tf_op jit(solution)/shard_map/dot_general | solution.py:229
  288.5 57.6 %convolution_bitcast_fusion.2 = f32[7168,256]{1,0:T(8,128)} fusion(bf16[8192,7168]{1,0:T(8,128)(2,1)} %param.2, bf16[256,8192]{1,0:T(8,128)(2,1)} %convolution_convert_fusion.2.clone.2), kind=kOutput, calls=%fused_computation.7 | convolution fusion | flops 30064771072 | bytes 128974848 | tf_op jit(solution)/shard_map/dot_general | solution.py:230
  346.1 0.0 reduce-scatter.7.cloned.1.call-update
  346.1 0.0 reduce-scatter.9.cloned.1.call-start
  346.1 58.0 %reduce-scatter.7.cloned.1.call-done.z_ref = f32[896,256]{1,0:T(8,128)} async-done(((f32[7168,256]{1,0:T(8,128)}), f32[896,256]{1,0:T(8,128)}) %reduce-scatter.7.cloned.1.call-update) | async-done | bytes 917520 | tf_op jit(solution)/shard_map/reduce_scatter | solution.py:231
  404.1 69.3 %orthonormalize.5 = (f32[896,256]{1,0:T(8,128)}, bf16[8,896,256]{2,1,0:T(8,128)(2,1)}) custom-call(f32[896,256]{1,0:T(8,128)} %reduce-scatter.7.cloned.1.call-done.z_ref), custom_call_target="tpu_custom_call" | custom-call | flops 4000000000 | bytes 6000000 | tf_op jit(solution)/shard_map/orthonormalize/pallas_call | solution.py:201
  473.5 45.7 %convolution_convert_fusion.1.clone.2 = bf16[256,8192]{1,0:T(8,128)(2,1)} fusion(bf16[7168,256]{1,0:T(8,128)(2,1)} %bitcast.48, bf16[8192,7168]{1,0:T(8,128)(2,1)} %param.2), kind=kOutput, calls=%fused_computation.2.clone.clone.clone | convolution fusion | flops 30066868224 | bytes 125304832 | tf_op jit(solution)/shard_map/dot_general | solution.py:229
  519.1 57.5 %convolution_bitcast_fusion.1 = f32[7168,256]{1,0:T(8,128)} fusion(bf16[8192,7168]{1,0:T(8,128)(2,1)} %param.2, bf16[256,8192]{1,0:T(8,128)(2,1)} %convolution_convert_fusion.1.clone.2), kind=kOutput, calls=%fused_computation.6 | convolution fusion | flops 30064771072 | bytes 128974848 | tf_op jit(solution)/shard_map/dot_general | solution.py:230
  576.7 0.0 reduce-scatter.9.cloned.1.call-update
  576.7 0.0 reduce-scatter.11.cloned.1.call-start
  576.7 58.0 %reduce-scatter.9.cloned.1.call-done.z_ref = f32[896,256]{1,0:T(8,128)} async-done(((f32[7168,256]{1,0:T(8,128)}), f32[896,256]{1,0:T(8,128)}) %reduce-scatter.9.cloned.1.call-update) | async-done | bytes 917520 | tf_op jit(solution)/shard_map/reduce_scatter | solution.py:231
  634.7 69.1 %orthonormalize.6 = (f32[896,256]{1,0:T(8,128)}, bf16[8,896,256]{2,1,0:T(8,128)(2,1)}) custom-call(f32[896,256]{1,0:T(8,128)} %reduce-scatter.9.cloned.1.call-done.z_ref), custom_call_target="tpu_custom_call" | custom-call | flops 4000000000 | bytes 6000000 | tf_op jit(solution)/shard_map/orthonormalize/pallas_call | solution.py:201
  703.8 45.7 %convolution_convert_fusion.clone.4 = bf16[256,8192]{1,0:T(8,128)(2,1)} fusion(bf16[7168,256]{1,0:T(8,128)(2,1)} %bitcast.49, bf16[8192,7168]{1,0:T(8,128)(2,1)} %param.2), kind=kOutput, calls=%fused_computation.1.clone.clone.clone.1 | convolution fusion | flops 30066868224 | bytes 125304832 | tf_op jit(solution)/shard_map/dot_general | solution.py:229
  749.5 57.6 %convolution_bitcast_fusion = f32[7168,256]{1,0:T(8,128)} fusion(bf16[8192,7168]{1,0:T(8,128)(2,1)} %param.2, bf16[256,8192]{1,0:T(8,128)(2,1)} %convolution_convert_fusion.clone.4), kind=kOutput, calls=%fused_computation.5 | convolution fusion | flops 30064771072 | bytes 128974848 | tf_op jit(solution)/shard_map/dot_general | solution.py:230
  807.1 0.0 reduce-scatter.11.cloned.1.call-update
  807.1 0.0 all-gather.2.cloned.1.call-start
  807.2 58.0 %reduce-scatter.11.cloned.1.call-done.z_ref = f32[896,256]{1,0:T(8,128)} async-done(((f32[7168,256]{1,0:T(8,128)}), f32[896,256]{1,0:T(8,128)}) %reduce-scatter.11.cloned.1.call-update) | async-done | bytes 917520 | tf_op jit(solution)/shard_map/reduce_scatter | solution.py:231
  865.2 69.2 %orthonormalize.7 = (f32[896,256]{1,0:T(8,128)}, bf16[8,896,256]{2,1,0:T(8,128)(2,1)}) custom-call(f32[896,256]{1,0:T(8,128)} %reduce-scatter.11.cloned.1.call-done.z_ref), custom_call_target="tpu_custom_call" | custom-call | flops 4000000000 | bytes 6000000 | tf_op jit(solution)/shard_map/orthonormalize/pallas_call | solution.py:201
  934.4 0.0 all-gather.2.cloned.1.call-update
  934.4 44.5 %fusion.3 = f32[256]{0:T(256)S(1)} fusion(bf16[7168,256]{1,0:T(8,128)(2,1)} %bitcast.46, bf16[8192,7168]{1,0:T(8,128)(2,1)} %param.2), kind=kOutput, calls=%fused_computation.10 | convolution fusion | flops 30068965376 | bytes 121111552 | tf_op jit(solution)/shard_map/dot_general | solution.py:235
  978.9 22.2 %psum.7 = f32[256]{0:T(256)} all-reduce(f32[256]{0:T(256)S(1)} %fusion.3), channel_id=1, replica_groups=mesh['batch'=1,'row'=2,'col'=4] {'row','col'}, use_global_device_ids=true, to_apply=%region_5.0 | all-reduce | flops 256 | bytes 2048 | tf_op jit(solution)/shard_map/psum | solution.py:236
  1001.2 0.0 all-gather.2.cloned.1.call-done
  1001.2 6.6 copy.13
Async XLA Ops:
  7.2 166.8 %reduce-scatter.5.cloned.1.call-start = ((), (), s32[]{:S(2)}) async-start(), calls=%async_computation.4 | async-start | bytes 8257536 | tf_op jit(solution)/shard_map/reduce_scatter | solution.py:231
  113.1 291.1 %reduce-scatter.7.cloned.1.call-start = ((), (), s32[]{:S(2)}) async-start(), calls=%async_computation.5 | async-start | bytes 8257536 | tf_op jit(solution)/shard_map/reduce_scatter | solution.py:231
  346.1 288.6 %reduce-scatter.9.cloned.1.call-start = ((), (), s32[]{:S(2)}) async-start(), calls=%async_computation.6 | async-start | bytes 8257536 | tf_op jit(solution)/shard_map/reduce_scatter | solution.py:231
  576.7 288.5 %reduce-scatter.11.cloned.1.call-start = ((), (), s32[]{:S(2)}) async-start(), calls=%async_computation.7 | async-start | bytes 8257536 | tf_op jit(solution)/shard_map/reduce_scatter | solution.py:231
  807.1 194.1 %all-gather.2.cloned.1.call-start = ((), (), s32[]{:S(2)}) async-start(), calls=%async_computation.8 | async-start | bytes 8257536 | tf_op jit(solution)/shard_map/all_gather | solution.py:234
Sparse Core Ops, SparseCore 0:
  113.2 60.6 reduce-scatter.4
  346.2 57.8 reduce-scatter.6
  576.8 57.8 reduce-scatter.8
  807.2 57.8 reduce-scatter.10
  934.5 43.9 all-gather.1

commit v2 on v1

--- a/solution.py
+++ b/solution.py
@@ -13,7 +13,9 @@
 MESH = pl.DeviceIdType.MESH
 HALF = 128
 PEERS = 7
-VMEM_BYTES = 60 * 1024 * 1024
+VMEM_BYTES = 63 * 1024 * 1024
+TILES = 8
+DEPTH = 6
 
 
 def exact_dot(left, right, dims):
@@ -85,11 +87,180 @@
             inv_low[HALF:, :HALF] = -exact_dot(block_inv, inv_low[HALF:, :HALF], PLAIN)
 
 
-def qr_kernel(z_ref, q_ref, all_ref, part, slots, gram, work, inv_low, sum_send, sum_recv, out_send, out_recv, cast_send, cast_recv):
+def sweep_kernel(data, basis, z_ref, ring, acc, proj_t, part, from_twin, from_far, from_side, ring_sem, twin_sem, far_sem, side_sem):
+    row, col = lax.axis_index("row"), lax.axis_index("col")
+    core, x = lax.rem(col, 2), col // 2
+    twin, x_side, y_side = (0, row, col + 1 - 2 * core), (0, row, core + 2 * (1 - x)), (0, 1 - row, col)
+    tile_rows, chip_cols, width = data.shape[0] // TILES, data.shape[1] // 4, basis.shape[1]
+    half, top = chip_cols // 2, width // 2
+    turns = 4 * TILES
+    skip = turns - DEPTH - 3 * TILES
+
+    def flip(bit, change):
+        return bit + change - 2 * bit * change
+
+    def chip_of(step):
+        return flip(row, step // 2) * 2 + flip(x, lax.rem(step, 2))
+
+    def fetch(turn, slot):
+        first = turn < turns
+        local = jnp.where(first, turn, turn - turns)
+        step = jnp.where(first, local // TILES, 3 - local // TILES)
+        place = jnp.where(first, lax.rem(local, TILES), lax.rem(local + skip, TILES))
+        rows = pl.ds(pl.multiple_of(place * tile_rows, tile_rows), tile_rows)
+        cols = pl.ds(pl.multiple_of(chip_of(step) * chip_cols, chip_cols), chip_cols)
+        return pltpu.make_async_copy(data.at[rows, cols], ring.at[slot], ring_sem.at[slot])
+
+    for turn in range(DEPTH):
+        fetch(turn, turn).start()
+    acc[...] = jnp.zeros_like(acc)
+    part[...] = jnp.zeros_like(part)
+
+    barrier = pltpu.get_barrier_semaphore()
+    for device in (twin, x_side, y_side):
+        pl.semaphore_signal(barrier, inc=1, device_id=device, device_id_type=MESH)
+    pl.semaphore_wait(barrier, 3)
+
+    @pl.loop(0, turns)
+    def _(turn):
+        slot = lax.rem(turn, DEPTH)
+        fetch(turn, slot).wait()
+        place = lax.rem(turn, TILES)
+        factor = pl.ds(pl.multiple_of(chip_of(turn // TILES) * chip_cols, chip_cols), chip_cols)
+
+        @pl.loop(0, 2)
+        def _(piece):
+            inner = pl.ds(pl.multiple_of(piece * (tile_rows // 2), tile_rows // 2), tile_rows // 2)
+            rows = pl.ds(pl.multiple_of(place * tile_rows + piece * (tile_rows // 2), tile_rows // 2), tile_rows // 2)
+            acc[rows, :] += jnp.dot(ring[slot, inner, :], basis[factor, :], preferred_element_type=jnp.float32)
+
+        @pl.when(turn + DEPTH < turns)
+        def _():
+            fetch(turn + DEPTH, slot).start()
+
+        @pl.when(turn >= 3 * TILES)
+        def _():
+            rows = pl.ds(pl.multiple_of(place * tile_rows, tile_rows), tile_rows)
+            proj_t[place] = acc[rows, :].astype(jnp.bfloat16).T
+
+    mine, other = pl.ds(pl.multiple_of(core * half, HALF), half), pl.ds(pl.multiple_of((1 - core) * half, HALF), half)
+    upper, lower = pl.ds(0, top), pl.ds(top, width - top)
+
+    def swap(chunk):
+        return pltpu.make_async_remote_copy(
+            src_ref=part.at[chunk, :, other], dst_ref=from_twin.at[chunk], send_sem=twin_sem.at[0, chunk], recv_sem=twin_sem.at[1, chunk], device_id=twin, device_id_type=MESH
+        )
+
+    def lift(chunk):
+        swap(chunk).wait_recv()
+        part[chunk, :, mine] = part[chunk, :, mine] + from_twin[chunk]
+
+    def relay(piece, which, device):
+        return pltpu.make_async_remote_copy(
+            src_ref=part.at[0, piece, mine], dst_ref=from_far.at[which], send_sem=far_sem.at[0, which], recv_sem=far_sem.at[1, which], device_id=device, device_id_type=MESH
+        )
+
+    def deliver(chunk, piece, which, device):
+        return pltpu.make_async_remote_copy(
+            src_ref=part.at[chunk, piece, mine], dst_ref=from_side.at[chunk - 1, piece], send_sem=side_sem.at[0, chunk - 1, which], recv_sem=side_sem.at[1, chunk - 1, which], device_id=device, device_id_type=MESH
+        )
+
+    far_to_x, far_to_y = relay(upper, 0, x_side), relay(lower, 1, y_side)
+    y_low, y_up = deliver(1, lower, 1, y_side), deliver(1, upper, 0, y_side)
+    x_up, x_low = deliver(2, upper, 0, x_side), deliver(2, lower, 1, x_side)
+
+    @pl.loop(0, turns)
+    def _(turn):
+        slot = lax.rem(turn + turns, DEPTH)
+
+        @pl.when(turn >= DEPTH)
+        def _():
+            fetch(turn + turns, slot).wait()
+
+        chunk, place = turn // TILES, lax.rem(turn + skip, TILES)
+        part[chunk] += jnp.dot(proj_t[place], ring[slot], preferred_element_type=jnp.float32)
+
+        @pl.when(turn + DEPTH < turns)
+        def _():
+            fetch(turn + turns + DEPTH, slot).start()
+
+        @pl.when(lax.rem(turn, TILES) == TILES - 1)
+        def _():
+            swap(chunk).start()
+
+        @pl.when(turn == TILES + 1)
+        def _():
+            lift(0)
+            far_to_x.start()
+            far_to_y.start()
+
+        @pl.when(turn == 2 * TILES + 1)
+        def _():
+            lift(1)
+            y_low.start()
+
+        @pl.when(turn == 2 * TILES + 5)
+        def _():
+            far_to_x.wait_recv()
+            part[1, upper, mine] = part[1, upper, mine] + from_far[0]
+            y_up.start()
+
+        @pl.when(turn == 3 * TILES + 1)
+        def _():
+            lift(2)
+            x_up.start()
+            far_to_y.wait_recv()
+            part[2, lower, mine] = part[2, lower, mine] + from_far[1]
+            x_low.start()
+
+    lift(3)
+    y_low.wait_recv()
+    y_up.wait_recv()
+    z_ref[...] = part[3, :, mine] + from_side[0]
+    x_up.wait_recv()
+    x_low.wait_recv()
+    z_ref[...] += from_side[1]
+    for chunk in range(4):
+        swap(chunk).wait_send()
+    for copy in (far_to_x, far_to_y, y_low, y_up, x_up, x_low):
+        copy.wait_send()
+
+
+def pull_rows(data_local, basis_low):
+    rows, features = data_local.shape
+    width = basis_low.shape[1]
+    tile_rows, chip_cols = rows // TILES, features // 4
+    half = chip_cols // 2
+    flops = 4 * rows * features * width
+    return pl.pallas_call(
+        sweep_kernel,
+        out_shape=jax.ShapeDtypeStruct((width, half), jnp.float32),
+        in_specs=[pl.BlockSpec(memory_space=pl.ANY), pl.BlockSpec(memory_space=pltpu.VMEM)],
+        out_specs=pl.BlockSpec(memory_space=pltpu.VMEM),
+        scratch_shapes=[
+            pltpu.VMEM((DEPTH, tile_rows, chip_cols), jnp.bfloat16),
+            pltpu.VMEM((rows, width), jnp.float32),
+            pltpu.VMEM((TILES, width, tile_rows), jnp.bfloat16),
+            pltpu.VMEM((4, width, chip_cols), jnp.float32),
+            pltpu.VMEM((4, width, half), jnp.float32),
+            pltpu.VMEM((2, width // 2, half), jnp.float32),
+            pltpu.VMEM((2, width, half), jnp.float32),
+            pltpu.SemaphoreType.DMA((DEPTH,)),
+            pltpu.SemaphoreType.DMA((2, 4)),
+            pltpu.SemaphoreType.DMA((2, 2)),
+            pltpu.SemaphoreType.DMA((2, 2, 2)),
+        ],
+        compiler_params=pltpu.CompilerParams(collective_id=1, has_side_effects=True, vmem_limit_bytes=VMEM_BYTES),
+        cost_estimate=pl.CostEstimate(flops=flops, bytes_accessed=4 * rows * features, transcendentals=0),
+        name="pull_rows",
+    )(data_local, basis_low)
+
+
+def qr_kernel(z_ref, q_ref, all_ref, turned, part, slots, gram, work, inv_low, sum_send, sum_recv, out_send, out_recv, cast_send, cast_recv):
     row, col = lax.axis_index("row"), lax.axis_index("col")
     me = row * 4 + col
     chunk = 3 * HALF // 8
-    rows = z_ref.shape[0]
+    rows = z_ref.shape[1]
 
     def peer(offset):
         other = lax.rem(me + offset, 8)
@@ -137,11 +308,11 @@
         for copy in spread:
             copy.wait()
 
-    z_left, z_right = z_ref[:, :HALF].astype(jnp.bfloat16), z_ref[:, HALF:].astype(jnp.bfloat16)
+    z_left, z_right = z_ref[:HALF, :].astype(jnp.bfloat16), z_ref[HALF:, :].astype(jnp.bfloat16)
     for place, (left, right) in enumerate(((z_left, z_left), (z_left, z_right), (z_right, z_right))):
-        part[0, HALF * place:HALF * (place + 1), :] = lax.dot_general(left, right, ROW_CONTRACT, preferred_element_type=jnp.float32)
-
-    q_ref[...] = z_ref[...]
+        part[0, HALF * place:HALF * (place + 1), :] = lax.dot_general(left, right, LANE_CONTRACT, preferred_element_type=jnp.float32)
+
+    turned[...] = z_ref[...]
 
     def turn_body(turn):
         share_gram(turn)
@@ -150,12 +321,12 @@
         @pl.loop(0, rows // HALF)
         def _(i):
             block = pl.ds(pl.multiple_of(i * HALF, HALF), HALF)
-            q_ref[block, :] = exact_dot(q_ref[block, :], inv_low[...], LANE_CONTRACT)
+            turned[:, block] = exact_dot(inv_low[...], turned[:, block], PLAIN)
 
         @pl.when(turn == 0)
         def _():
             for place, (left, right) in enumerate(((0, 0), (0, HALF), (HALF, HALF))):
-                part[1, HALF * place:HALF * (place + 1), :] = exact_dot(q_ref[:, left:left + HALF], q_ref[:, right:right + HALF], ROW_CONTRACT)
+                part[1, HALF * place:HALF * (place + 1), :] = exact_dot(turned[left:left + HALF, :], turned[right:right + HALF, :], LANE_CONTRACT)
 
     pl.loop(0, 2)(turn_body)
 
@@ -164,7 +335,13 @@
     x_index, y_index, far_index = row * 4 + x_side[2], (1 - row) * 4 + col, (1 - row) * 4 + x_side[2]
     upper, lower = pl.ds(0, rows // 2), pl.ds(rows // 2, rows // 2)
     whole = pl.ds(0, rows)
-    all_ref[me] = q_ref[...].astype(jnp.bfloat16)
+
+    @pl.loop(0, rows // HALF)
+    def _(i):
+        block = pl.ds(pl.multiple_of(i * HALF, HALF), HALF)
+        q_ref[block, :] = turned[:, block].T
+        all_ref[me, block, :] = q_ref[block, :].astype(jnp.bfloat16)
+
 
     def hand(slot, owner, piece, device):
         copy = pltpu.make_async_remote_copy(
@@ -197,13 +374,14 @@
 
 
 def orthonormalize(z_rows):
-    rows, width = z_rows.shape
+    width, rows = z_rows.shape
     return pl.pallas_call(
         qr_kernel,
         out_shape=(jax.ShapeDtypeStruct((rows, width), jnp.float32), jax.ShapeDtypeStruct((8, rows, width), jnp.bfloat16)),
         in_specs=[pl.BlockSpec(memory_space=pltpu.VMEM)],
         out_specs=(pl.BlockSpec(memory_space=pltpu.VMEM), pl.BlockSpec(memory_space=pltpu.VMEM)),
         scratch_shapes=[
+            pltpu.VMEM((width, rows), jnp.float32),
             pltpu.VMEM((2, 3 * HALF, HALF), jnp.float32),
             pltpu.VMEM((2, PEERS, 3 * HALF // 8, HALF), jnp.float32),
             pltpu.VMEM((2, 3 * HALF, HALF), jnp.float32),
@@ -226,9 +404,7 @@
     def device_sweeps(data_local, start_block):
         basis_low = start_block.astype(jnp.bfloat16)
         for _ in range(SWEEPS):
-            projected = jnp.dot(data_local, basis_low, preferred_element_type=jnp.float32).astype(jnp.bfloat16)
-            pulled_part = lax.dot_general(data_local, projected, ROW_CONTRACT, preferred_element_type=jnp.float32)
-            pulled_rows = lax.psum_scatter(pulled_part, GROUP_AXES, scatter_dimension=0, tiled=True)
+            pulled_rows = pull_rows(data_local, basis_low)
             q_rows, basis_blocks = orthonormalize(pulled_rows)
             basis_low = basis_blocks.reshape(start_block.shape)
         q_basis = lax.all_gather(q_rows, GROUP_AXES, axis=0, tiled=True)

time: 1020 us -> 789 us (0.77)
  matrix products: 460 us -> 44.5 us
  Pallas kernels: 276 us -> 686 us
  waiting for transfers between devices: 235 us -> 0.02 us
    pallas_call x0 -> x4, Pallas kernels: none -> 410 us  [pull_rows(): pl.pallas_call(sweep_kernel, out_shape=jax.ShapeDtypeStruct((width, half)...]
    reduce_scatter x4 -> x0, waiting for transfers between devices: 235 us -> none  [device_sweeps(): lax.psum_scatter(pulled_part, GROUP_AXES, scatter_dimension=0, tiled=True)]
    dot_general x4 -> x0, matrix products: 233 us -> none  [device_sweeps(): lax.dot_general(data_local, projected, ROW_CONTRACT, preferred_element_ty...]
    dot_general x5 -> x1, matrix products: 227 us -> 44.5 us  [device_sweeps(): jnp.dot(data_local, basis_low, preferred_element_type=jnp.float32)]
  transfers between devices with their start and end apart: 5 -> 1, of which waited for: 4 -> 0; matrix products, arithmetic and copies ran while one was open for 4% -> 6% of each run, Pallas kernels for 0% -> 0%
where the time goes in v2:
time: 789 us; the launch traced here: 779 us
  Pallas kernels  686 us (87%)
  matrix products  44.5 us (6%)
  blocking collectives  22.3 us (3%)
  between operations  14.5 us (2%)
    pallas_call x4, Pallas kernels, pull_rows(): pl.pallas_call(sweep_kernel, out_shape=jax.ShapeDtypeStruct((width, half)...  410 us
    pallas_call x4, Pallas kernels, orthonormalize(): pl.pallas_call(qr_kernel, out_shape=(jax.ShapeDtypeStruct((rows, width),...  276 us
    dot_general x1, matrix products, device_sweeps(): jnp.dot(data_local, basis_low, preferred_element_type=jnp.float32)  44.5 us
    psum x1, blocking collectives, device_sweeps(): ritz_vals = lax.psum(jnp.sum(final_proj * final_proj, axis=0), GROUP_AXES)  22.3 us
  transfers between devices with their start and end apart: 1, of which 0 were waited for; matrix products, arithmetic and copies ran while one was open for 6% of the time, Pallas kernels for 0%

profile of v2, /device:TPU:0, one launch (start us, length us, event | category | flops | bytes accessed | tf_op | source)
XLA Modules:
  0.0 779.2 jit_solution(5698392285713369482)
XLA Ops:
  7.2 0.0 all-gather.2.cloned.1.call-start
  7.2 5.3 convert_element_type.3.basis
  12.5 104.4 %pull_rows.4.z_ref = f32[256,896]{1,0:T(8,128)} custom-call(bf16[8192,7168]{1,0:T(8,128)(2,1)} %data.7, bf16[7168,256]{1,0:T(8,128)(2,1)} %convert_element_type.3.basis), custom_call_target="tpu_custom_call" | custom-call | flops 60129542144 | bytes 234881024 | tf_op jit(solution)/shard_map/pull_rows/pallas_call | solution.py:235
  116.9 68.8 %orthonormalize.4 = (f32[896,256]{1,0:T(8,128)}, bf16[8,896,256]{2,1,0:T(8,128)(2,1)}) custom-call(f32[256,896]{1,0:T(8,128)} %pull_rows.4.z_ref), custom_call_target="tpu_custom_call" | custom-call | flops 4000000000 | bytes 6000000 | tf_op jit(solution)/shard_map/orthonormalize/pallas_call | solution.py:378
  185.7 101.9 %pull_rows.5.z_ref = f32[256,896]{1,0:T(8,128)} custom-call(bf16[8192,7168]{1,0:T(8,128)(2,1)} %data.7, bf16[7168,256]{1,0:T(8,128)(2,1)} %bitcast.7), custom_call_target="tpu_custom_call" | custom-call | flops 60129542144 | bytes 234881024 | tf_op jit(solution)/shard_map/pull_rows/pallas_call | solution.py:235
  287.6 69.0 %orthonormalize.5 = (f32[896,256]{1,0:T(8,128)}, bf16[8,896,256]{2,1,0:T(8,128)(2,1)}) custom-call(f32[256,896]{1,0:T(8,128)} %pull_rows.5.z_ref), custom_call_target="tpu_custom_call" | custom-call | flops 4000000000 | bytes 6000000 | tf_op jit(solution)/shard_map/orthonormalize/pallas_call | solution.py:378
  356.6 101.9 %pull_rows.6.z_ref = f32[256,896]{1,0:T(8,128)} custom-call(bf16[8192,7168]{1,0:T(8,128)(2,1)} %data.7, bf16[7168,256]{1,0:T(8,128)(2,1)} %bitcast.8), custom_call_target="tpu_custom_call" | custom-call | flops 60129542144 | bytes 234881024 | tf_op jit(solution)/shard_map/pull_rows/pallas_call | solution.py:235
  458.5 69.0 %orthonormalize.6 = (f32[896,256]{1,0:T(8,128)}, bf16[8,896,256]{2,1,0:T(8,128)(2,1)}) custom-call(f32[256,896]{1,0:T(8,128)} %pull_rows.6.z_ref), custom_call_target="tpu_custom_call" | custom-call | flops 4000000000 | bytes 6000000 | tf_op jit(solution)/shard_map/orthonormalize/pallas_call | solution.py:378
  527.5 101.9 %pull_rows.7.z_ref = f32[256,896]{1,0:T(8,128)} custom-call(bf16[8192,7168]{1,0:T(8,128)(2,1)} %data.7, bf16[7168,256]{1,0:T(8,128)(2,1)} %bitcast.9), custom_call_target="tpu_custom_call" | custom-call | flops 60129542144 | bytes 234881024 | tf_op jit(solution)/shard_map/pull_rows/pallas_call | solution.py:235
  629.4 69.2 %orthonormalize.7 = (f32[896,256]{1,0:T(8,128)}, bf16[8,896,256]{2,1,0:T(8,128)(2,1)}) custom-call(f32[256,896]{1,0:T(8,128)} %pull_rows.7.z_ref), custom_call_target="tpu_custom_call" | custom-call | flops 4000000000 | bytes 6000000 | tf_op jit(solution)/shard_map/orthonormalize/pallas_call | solution.py:378
  698.5 0.0 all-gather.2.cloned.1.call-update
  698.6 44.5 %fusion = f32[256]{0:T(256)S(1)} fusion(bf16[7168,256]{1,0:T(8,128)(2,1)} %bitcast.6, bf16[8192,7168]{1,0:T(8,128)(2,1)} %data.7), kind=kOutput, calls=%fused_computation.1 | convolution fusion | flops 30068965376 | bytes 121111552 | tf_op jit(solution)/shard_map/dot_general | solution.py:411
  743.1 22.3 %psum.7 = f32[256]{0:T(256)} all-reduce(f32[256]{0:T(256)S(1)} %fusion), channel_id=1, replica_groups=mesh['batch'=1,'row'=2,'col'=4] {'row','col'}, use_global_device_ids=true, to_apply=%region_1.0 | all-reduce | flops 256 | bytes 2048 | tf_op jit(solution)/shard_map/psum | solution.py:412
  765.4 0.0 all-gather.2.cloned.1.call-done
  765.4 6.6 copy.5
Async XLA Ops:
  7.2 758.2 %all-gather.2.cloned.1.call-start = ((), (), s32[]{:S(2)}) async-start(), calls=%async_computation | async-start | bytes 8257536 | tf_op jit(solution)/shard_map/all_gather | solution.py:410
Sparse Core Ops, SparseCore 0:
  698.7 43.9 all-gather.1

commit v3 on v1

--- a/solution.py
+++ b/solution.py
@@ -6,14 +6,15 @@
 from jax.sharding import PartitionSpec as P
 
 SWEEPS = 4
-GROUP_AXES = ("row", "col")
 ROW_CONTRACT = (((0,), (0,)), ((), ()))
 LANE_CONTRACT = (((1,), (1,)), ((), ()))
 PLAIN = (((1,), (0,)), ((), ()))
 MESH = pl.DeviceIdType.MESH
 HALF = 128
 PEERS = 7
-VMEM_BYTES = 60 * 1024 * 1024
+VMEM_BYTES = 63 * 1024 * 1024
+TILES = 8
+DEPTH = 8
 
 
 def exact_dot(left, right, dims):
@@ -85,11 +86,348 @@
             inv_low[HALF:, :HALF] = -exact_dot(block_inv, inv_low[HALF:, :HALF], PLAIN)
 
 
-def qr_kernel(z_ref, q_ref, all_ref, part, slots, gram, work, inv_low, sum_send, sum_recv, out_send, out_recv, cast_send, cast_recv):
+def cut_of(chip_cols):
+    first = 2 * HALF * ((chip_cols // (2 * HALF) + 1) // 2)
+    return first, chip_cols - first
+
+
+class Place:
+    def __init__(self, features):
+        self.row, self.col = lax.axis_index("row"), lax.axis_index("col")
+        self.core, self.x = lax.rem(self.col, 2), self.col // 2
+        self.twin = (0, self.row, self.col + 1 - 2 * self.core)
+        self.x_side = (0, self.row, self.core + 2 * (1 - self.x))
+        self.y_side = (0, 1 - self.row, self.col)
+        self.chip_cols = features // 4
+        self.widths = cut_of(self.chip_cols)
+
+    def chip(self, flip_x, flip_y):
+        x = self.x + flip_x - 2 * self.x * flip_x
+        y = self.row + flip_y - 2 * self.row * flip_y
+        return y * 2 + x
+
+    def columns(self, flip_x, flip_y, sub):
+        start = self.chip(flip_x, flip_y) * self.chip_cols + sub * self.widths[0]
+        return pl.ds(pl.multiple_of(start, 2 * HALF), self.widths[sub])
+
+    def owned(self, flip_x, flip_y, sub):
+        start = self.chip(flip_x, flip_y) * self.chip_cols + sub * self.widths[0] + self.core * (self.widths[sub] // 2)
+        return pl.ds(pl.multiple_of(start, HALF), self.widths[sub] // 2)
+
+
+def as_int(flag):
+    return jnp.where(flag, 1, 0)
+
+
+def first_order(block):
+    far = block >= 6
+    in_x = (block == 2) | (block == 4) | far
+    in_y = (block == 3) | (block == 5) | far
+    return as_int(in_x), as_int(in_y), as_int((block == 1) | ((block >= 4) & (block <= 6)))
+
+
+def second_order(block):
+    far = block < 2
+    in_x = far | (block == 3) | (block == 5)
+    in_y = far | (block == 2) | (block == 4)
+    return as_int(in_x), as_int(in_y), as_int((block == 1) | (block == 4) | (block == 5) | (block == 7))
+
+
+def by_width(sub, action):
+    for static in range(2):
+        pl.when(sub == static)(lambda static=static: action(static))
+
+
+def tile_copy(place, data, ring, ring_sem, tile, slot, order, begin):
+    flip_x, flip_y, sub = order(tile // TILES)
+    tile_rows = ring.shape[1]
+    rows = pl.ds(pl.multiple_of(lax.rem(tile, TILES) * tile_rows, tile_rows), tile_rows)
+
+    def act(static):
+        copy = pltpu.make_async_copy(data.at[rows, place.columns(flip_x, flip_y, static)], ring.at[slot, :, pl.ds(0, place.widths[static])], ring_sem.at[slot])
+        copy.start() if begin else copy.wait()
+
+    by_width(sub, act)
+
+
+def first_pass(place, data, own, landing, basis, ring, acc, ring_sem, gather_sem, clear, finish, after):
+    turns = 8 * TILES
+    tile_rows = ring.shape[1]
+    for turn in range(DEPTH):
+        tile_copy(place, data, ring, ring_sem, turn, turn, first_order, True)
+
+    barrier = pltpu.get_barrier_semaphore()
+    for offset in range(1, 8):
+        other = lax.rem(place.row * 4 + place.col + offset, 8)
+        pl.semaphore_signal(barrier, inc=1, device_id=(0, other // 4, lax.rem(other, 4)), device_id_type=MESH)
+    pl.semaphore_wait(barrier, PEERS)
+
+    piece = (pl.ds(0, place.widths[0] // 2), pl.ds(place.widths[0] // 2, place.widths[1] // 2))
+
+    def hand(index, flip_x, flip_y, sub, device):
+        rows = place.owned(flip_x, flip_y, sub)
+        source = own.at[piece[sub]] if flip_x + flip_y == 0 else landing.at[rows]
+        return pltpu.make_async_remote_copy(
+            src_ref=source, dst_ref=landing.at[rows], send_sem=gather_sem.at[0, index], recv_sem=gather_sem.at[1, index], device_id=device, device_id_type=MESH
+        )
+
+    twin, x_side, y_side = place.twin, place.x_side, place.y_side
+    copies = [
+        hand(0, 0, 0, 0, x_side), hand(1, 0, 0, 0, y_side), hand(2, 0, 0, 0, twin),
+        hand(3, 0, 0, 1, x_side), hand(4, 0, 0, 1, y_side), hand(5, 0, 0, 1, twin),
+        hand(6, 1, 0, 0, y_side), hand(7, 1, 0, 0, twin), hand(8, 1, 0, 1, twin),
+        hand(9, 0, 1, 1, x_side), hand(10, 0, 1, 0, twin), hand(11, 0, 1, 1, twin),
+        hand(12, 1, 1, 0, twin), hand(13, 1, 1, 1, twin),
+    ]
+    for index in range(6):
+        copies[index].start()
+    for sub in range(2):
+        landing[place.owned(0, 0, sub), :] = own[piece[sub], :]
+    acc[...] = jnp.zeros_like(acc)
+    clear()
+
+    def at(turn, when, waits, starts):
+        @pl.when(turn == when)
+        def _():
+            for index in waits:
+                copies[index].wait_recv()
+            for index in starts:
+                copies[index].start()
+
+    @pl.loop(0, turns)
+    def _(turn):
+        at(turn, 0, (2,), ())
+        at(turn, TILES, (5,), ())
+        at(turn, 2 * TILES, (0,), (6, 7))
+        at(turn, 2 * TILES, (1,), (10,))
+        at(turn, 2 * TILES, (7,), ())
+        at(turn, 3 * TILES, (10,), ())
+        at(turn, 3 * TILES + 4, (3, 4), (8, 9, 11))
+        at(turn, 4 * TILES, (8,), ())
+        at(turn, 5 * TILES, (11,), ())
+        at(turn, 6 * TILES - 1, (9, 6), (13, 12))
+        at(turn, 6 * TILES, (13,), ())
+        at(turn, 7 * TILES, (12,), ())
+        slot = lax.rem(turn, DEPTH)
+        flip_x, flip_y, sub = first_order(turn // TILES)
+        tile_copy(place, data, ring, ring_sem, turn, slot, first_order, False)
+        part_rows = tile_rows // 2
+
+        def project(static):
+            cols = place.columns(flip_x, flip_y, static)
+            if landing is not basis:
+                @pl.when(lax.rem(turn, TILES) == 0)
+                def _():
+                    basis[cols, :] = landing[cols, :].astype(jnp.bfloat16)
+            for half in range(2):
+                inner = pl.ds(half * part_rows, part_rows)
+                rows = pl.ds(pl.multiple_of(lax.rem(turn, TILES) * tile_rows + half * part_rows, part_rows), part_rows)
+                acc[rows, :] += jnp.dot(ring[slot, inner, pl.ds(0, place.widths[static])], basis[cols, :], preferred_element_type=jnp.float32)
+
+        by_width(sub, project)
+
+        @pl.when(turn + DEPTH < turns)
+        def _():
+            tile_copy(place, data, ring, ring_sem, turn + DEPTH, slot, first_order, True)
+
+        @pl.when(turn >= turns - TILES)
+        def _():
+            tile = lax.rem(turn, TILES)
+            finish(tile, acc[pl.ds(pl.multiple_of(tile * tile_rows, tile_rows), tile_rows), :])
+
+    after()
+    for copy in copies:
+        copy.wait_send()
+
+
+def pull_kernel(data, own, z_ref, basis, ring, acc, proj_t, part0, part1, twin0, twin1, far0, far1, side0, side1, ring_sem, gather_sem, twin_sem, far_sem, side_sem):
+    place = Place(data.shape[1])
+    twin, x_side, y_side = place.twin, place.x_side, place.y_side
+    part, from_twin, from_far, from_side = (part0, part1), (twin0, twin1), (far0, far1), (side0, side1)
+    halves = tuple(width // 2 for width in place.widths)
+    width = z_ref.shape[0]
+    top = width // 2
+    turns = 8 * TILES
+
+    def clear():
+        part0[...] = jnp.zeros_like(part0)
+        part1[...] = jnp.zeros_like(part1)
+
+    def finish(tile, rows):
+        proj_t[tile] = rows.astype(jnp.bfloat16).T
+
+    first_pass(place, data, own, basis, basis, ring, acc, ring_sem, gather_sem, clear, finish, lambda: None)
+
+    upper, lower = pl.ds(0, top), pl.ds(top, width - top)
+    mine = tuple(pl.ds(pl.multiple_of(place.core * half, HALF), half) for half in halves)
+    other = tuple(pl.ds(pl.multiple_of((1 - place.core) * half, HALF), half) for half in halves)
+    FAR, Y, X, OWN = 0, 1, 2, 3
+
+    def remote(source, target, sems, device):
+        return pltpu.make_async_remote_copy(src_ref=source, dst_ref=target, send_sem=sems.at[0], recv_sem=sems.at[1], device_id=device, device_id_type=MESH)
+
+    swaps, relays, delivers = {}, {}, {}
+    for sub in range(2):
+        for kind in range(4):
+            swaps[kind, sub] = remote(part[sub].at[kind, :, other[sub]], from_twin[sub].at[kind], twin_sem.at[kind, sub], twin)
+        relays[0, sub] = remote(part[sub].at[FAR, upper, mine[sub]], from_far[sub].at[0], far_sem.at[0, sub], x_side)
+        relays[1, sub] = remote(part[sub].at[FAR, lower, mine[sub]], from_far[sub].at[1], far_sem.at[1, sub], y_side)
+        for kind, device in ((Y, y_side), (X, x_side)):
+            for which, rows in ((0, upper), (1, lower)):
+                delivers[kind, which, sub] = remote(part[sub].at[kind, rows, mine[sub]], from_side[sub].at[kind - 1, rows], side_sem.at[kind - 1, which, sub], device)
+
+    def lift(kind, sub):
+        swaps[kind, sub].wait_recv()
+        part[sub][kind, :, mine[sub]] = part[sub][kind, :, mine[sub]] + from_twin[sub][kind]
+
+    def send_far(sub):
+        lift(FAR, sub)
+        relays[0, sub].start()
+        relays[1, sub].start()
+
+    def send_side(kind, sub):
+        lift(kind, sub)
+        plain, joined, rows = (1, 0, upper) if kind == Y else (0, 1, lower)
+        delivers[kind, plain, sub].start()
+        relays[joined, sub].wait_recv()
+        part[sub][kind, rows, mine[sub]] = part[sub][kind, rows, mine[sub]] + from_far[sub][joined]
+        delivers[kind, joined, sub].start()
+
+    order = ((FAR, 0), (FAR, 1), (Y, 0), (X, 0), (Y, 1), (X, 1), (OWN, 0), (OWN, 1))
+
+    @pl.loop(0, turns)
+    def _(turn):
+        slot = lax.rem(turn, DEPTH)
+        block, tile = turn // TILES, lax.rem(turn, TILES)
+        sub = second_order(block)[2]
+
+        @pl.when(turn >= DEPTH)
+        def _():
+            tile_copy(place, data, ring, ring_sem, turn, slot, second_order, False)
+
+        kind = jnp.where(block < 2, FAR, jnp.where(block >= 6, OWN, jnp.where((block == 2) | (block == 4), Y, X)))
+
+        def pull(static):
+            part[static][kind] += jnp.dot(proj_t[tile], ring[slot, :, pl.ds(0, place.widths[static])], preferred_element_type=jnp.float32)
+
+        by_width(sub, pull)
+
+        @pl.when(turn + DEPTH < turns)
+        def _():
+            tile_copy(place, data, ring, ring_sem, turn + DEPTH, slot, second_order, True)
+
+        for index, (held, held_sub) in enumerate(order):
+            pl.when(turn == (index + 1) * TILES - 1)(lambda held=held, held_sub=held_sub: swaps[held, held_sub].start())
+            if held == FAR:
+                pl.when(turn == (index + 1) * TILES + 2)(lambda held_sub=held_sub: send_far(held_sub))
+            elif held != OWN:
+                pl.when(turn == (index + 1) * TILES + 3)(lambda held=held, held_sub=held_sub: send_side(held, held_sub))
+
+    for sub in range(2):
+        lanes = pl.ds(sub * halves[0], halves[sub])
+        lift(OWN, sub)
+        for kind in (Y, X):
+            for which in range(2):
+                delivers[kind, which, sub].wait_recv()
+        z_ref[:, lanes] = (part[sub][OWN, :, mine[sub]] + from_side[sub][0]) + from_side[sub][1]
+    for copy in (*swaps.values(), *relays.values(), *delivers.values()):
+        copy.wait_send()
+
+
+def ritz_kernel(data, own, q_ref, r_ref, basis, ring, acc, slots, ring_sem, gather_sem, share_sem):
+    place = Place(data.shape[1])
+    me = place.row * 4 + place.col
+    width = q_ref.shape[1]
+
+    def clear():
+        slots[me] = jnp.zeros((8, width), jnp.float32)
+
+    def finish(tile, rows):
+        slots[me] += jnp.sum((rows * rows).reshape(rows.shape[0] // 8, 8, width), axis=0)
+
+    def after():
+        sends = []
+        for offset in range(1, 8):
+            other = lax.rem(me + offset, 8)
+            copy = pltpu.make_async_remote_copy(
+                src_ref=slots.at[me], dst_ref=slots.at[me], send_sem=share_sem.at[0, offset - 1], recv_sem=share_sem.at[1, offset - 1],
+                device_id=(0, other // 4, lax.rem(other, 4)), device_id_type=MESH,
+            )
+            copy.start()
+            sends.append(copy)
+        for copy in sends:
+            copy.wait()
+        total = slots[0]
+        for index in range(1, 8):
+            total = total + slots[index]
+        r_ref[...] = jnp.sum(total, axis=0, keepdims=True)
+
+    first_pass(place, data, own, q_ref, basis, ring, acc, ring_sem, gather_sem, clear, finish, after)
+
+
+def stream_scratch(rows, features, width):
+    return [
+        pltpu.VMEM((features, width), jnp.bfloat16),
+        pltpu.VMEM((DEPTH, rows // TILES, cut_of(features // 4)[0]), jnp.bfloat16),
+        pltpu.VMEM((rows, width), jnp.float32),
+    ]
+
+
+def pull_rows(data_local, own):
+    rows, features = data_local.shape
+    width = own.shape[1]
+    widths = cut_of(features // 4)
+    pairs = []
+    for shape in ((4, width), (4, width), (2, width // 2), (2, width)):
+        scale = 1 if not pairs else 2
+        pairs += [pltpu.VMEM((*shape, size // scale), jnp.float32) for size in widths]
+    return pl.pallas_call(
+        pull_kernel,
+        out_shape=jax.ShapeDtypeStruct((width, features // 8), jnp.float32),
+        in_specs=[pl.BlockSpec(memory_space=pl.ANY), pl.BlockSpec(memory_space=pltpu.VMEM)],
+        out_specs=pl.BlockSpec(memory_space=pltpu.VMEM),
+        scratch_shapes=[
+            *stream_scratch(rows, features, width),
+            pltpu.VMEM((TILES, width, rows // TILES), jnp.bfloat16),
+            *pairs,
+            pltpu.SemaphoreType.DMA((DEPTH,)),
+            pltpu.SemaphoreType.DMA((2, 14)),
+            pltpu.SemaphoreType.DMA((4, 2, 2)),
+            pltpu.SemaphoreType.DMA((2, 2, 2)),
+            pltpu.SemaphoreType.DMA((2, 2, 2, 2)),
+        ],
+        compiler_params=pltpu.CompilerParams(collective_id=1, has_side_effects=True, vmem_limit_bytes=VMEM_BYTES),
+        cost_estimate=pl.CostEstimate(flops=4 * rows * features * width, bytes_accessed=4 * rows * features, transcendentals=0),
+        name="pull_rows",
+    )(data_local, own)
+
+
+def ritz(data_local, own):
+    rows, features = data_local.shape
+    width = own.shape[1]
+    return pl.pallas_call(
+        ritz_kernel,
+        out_shape=(jax.ShapeDtypeStruct((features, width), jnp.float32), jax.ShapeDtypeStruct((1, width), jnp.float32)),
+        in_specs=[pl.BlockSpec(memory_space=pl.ANY), pl.BlockSpec(memory_space=pltpu.VMEM)],
+        out_specs=(pl.BlockSpec(memory_space=pltpu.VMEM), pl.BlockSpec(memory_space=pltpu.VMEM)),
+        scratch_shapes=[
+            *stream_scratch(rows, features, width),
+            pltpu.VMEM((8, 8, width), jnp.float32),
+            pltpu.SemaphoreType.DMA((DEPTH,)),
+            pltpu.SemaphoreType.DMA((2, 14)),
+            pltpu.SemaphoreType.DMA((2, 7)),
+        ],
+        compiler_params=pltpu.CompilerParams(collective_id=2, has_side_effects=True, vmem_limit_bytes=VMEM_BYTES),
+        cost_estimate=pl.CostEstimate(flops=2 * rows * features * width, bytes_accessed=2 * rows * features, transcendentals=0),
+        name="ritz",
+    )(data_local, own)
+
+
+def qr_kernel(z_ref, q_ref, low_ref, turned, part, slots, gram, work, inv_low, sum_send, sum_recv, out_send, out_recv):
     row, col = lax.axis_index("row"), lax.axis_index("col")
     me = row * 4 + col
     chunk = 3 * HALF // 8
-    rows = z_ref.shape[0]
+    rows = z_ref.shape[1]
 
     def peer(offset):
         other = lax.rem(me + offset, 8)
@@ -137,11 +475,11 @@
         for copy in spread:
             copy.wait()
 
-    z_left, z_right = z_ref[:, :HALF].astype(jnp.bfloat16), z_ref[:, HALF:].astype(jnp.bfloat16)
+    z_left, z_right = z_ref[:HALF, :].astype(jnp.bfloat16), z_ref[HALF:, :].astype(jnp.bfloat16)
     for place, (left, right) in enumerate(((z_left, z_left), (z_left, z_right), (z_right, z_right))):
-        part[0, HALF * place:HALF * (place + 1), :] = lax.dot_general(left, right, ROW_CONTRACT, preferred_element_type=jnp.float32)
-
-    q_ref[...] = z_ref[...]
+        part[0, HALF * place:HALF * (place + 1), :] = lax.dot_general(left, right, LANE_CONTRACT, preferred_element_type=jnp.float32)
+
+    turned[...] = z_ref[...]
 
     def turn_body(turn):
         share_gram(turn)
@@ -150,60 +488,31 @@
         @pl.loop(0, rows // HALF)
         def _(i):
             block = pl.ds(pl.multiple_of(i * HALF, HALF), HALF)
-            q_ref[block, :] = exact_dot(q_ref[block, :], inv_low[...], LANE_CONTRACT)
+            turned[:, block] = exact_dot(inv_low[...], turned[:, block], PLAIN)
 
         @pl.when(turn == 0)
         def _():
             for place, (left, right) in enumerate(((0, 0), (0, HALF), (HALF, HALF))):
-                part[1, HALF * place:HALF * (place + 1), :] = exact_dot(q_ref[:, left:left + HALF], q_ref[:, right:right + HALF], ROW_CONTRACT)
+                part[1, HALF * place:HALF * (place + 1), :] = exact_dot(turned[left:left + HALF, :], turned[right:right + HALF, :], LANE_CONTRACT)
 
     pl.loop(0, 2)(turn_body)
 
-    core, x = lax.rem(col, 2), col // 2
-    twin, x_side, y_side = (0, row, col + 1 - 2 * core), (0, row, core + 2 * (1 - x)), (0, 1 - row, col)
-    x_index, y_index, far_index = row * 4 + x_side[2], (1 - row) * 4 + col, (1 - row) * 4 + x_side[2]
-    upper, lower = pl.ds(0, rows // 2), pl.ds(rows // 2, rows // 2)
-    whole = pl.ds(0, rows)
-    all_ref[me] = q_ref[...].astype(jnp.bfloat16)
-
-    def hand(slot, owner, piece, device):
-        copy = pltpu.make_async_remote_copy(
-            src_ref=all_ref.at[owner, piece],
-            dst_ref=all_ref.at[owner, piece],
-            send_sem=cast_send.at[slot],
-            recv_sem=cast_recv.at[slot],
-            device_id=device,
-            device_id_type=MESH,
-        )
-        copy.start()
-        return copy
-
-    from_x = hand(0, me, whole, x_side)
-    from_y = hand(1, me, whole, y_side)
-    from_twin = hand(2, me, whole, twin)
-    from_x.wait_recv()
-    far_y = hand(3, x_index, upper, y_side)
-    twin_x = hand(4, x_index, whole, twin)
-    from_y.wait_recv()
-    far_x = hand(5, y_index, lower, x_side)
-    twin_y = hand(6, y_index, whole, twin)
-    far_y.wait_recv()
-    far_x.wait_recv()
-    twin_far = hand(7, far_index, whole, twin)
-    for copy in (from_twin, twin_x, twin_y, twin_far):
-        copy.wait_recv()
-    for copy in (from_x, from_y, from_twin, far_y, far_x, twin_x, twin_y, twin_far):
-        copy.wait_send()
+    @pl.loop(0, rows // HALF)
+    def _(i):
+        block = pl.ds(pl.multiple_of(i * HALF, HALF), HALF)
+        q_ref[block, :] = turned[:, block].T
+        low_ref[block, :] = q_ref[block, :].astype(jnp.bfloat16)
 
 
 def orthonormalize(z_rows):
-    rows, width = z_rows.shape
+    width, rows = z_rows.shape
     return pl.pallas_call(
         qr_kernel,
-        out_shape=(jax.ShapeDtypeStruct((rows, width), jnp.float32), jax.ShapeDtypeStruct((8, rows, width), jnp.bfloat16)),
+        out_shape=(jax.ShapeDtypeStruct((rows, width), jnp.float32), jax.ShapeDtypeStruct((rows, width), jnp.bfloat16)),
         in_specs=[pl.BlockSpec(memory_space=pltpu.VMEM)],
         out_specs=(pl.BlockSpec(memory_space=pltpu.VMEM), pl.BlockSpec(memory_space=pltpu.VMEM)),
         scratch_shapes=[
+            pltpu.VMEM((width, rows), jnp.float32),
             pltpu.VMEM((2, 3 * HALF, HALF), jnp.float32),
             pltpu.VMEM((2, PEERS, 3 * HALF // 8, HALF), jnp.float32),
             pltpu.VMEM((2, 3 * HALF, HALF), jnp.float32),
@@ -213,8 +522,6 @@
             pltpu.SemaphoreType.DMA((2, PEERS)),
             pltpu.SemaphoreType.DMA((2, PEERS)),
             pltpu.SemaphoreType.DMA((2, PEERS)),
-            pltpu.SemaphoreType.DMA((8,)),
-            pltpu.SemaphoreType.DMA((8,)),
         ],
         compiler_params=pltpu.CompilerParams(collective_id=0, has_side_effects=True),
         cost_estimate=pl.CostEstimate(flops=4 * 10**9, bytes_accessed=6 * 10**6, transcendentals=0),
@@ -224,16 +531,15 @@
 
 def solution(mesh):
     def device_sweeps(data_local, start_block):
-        basis_low = start_block.astype(jnp.bfloat16)
+        chip_cols = start_block.shape[0] // 4
+        row, col = lax.axis_index("row"), lax.axis_index("col")
+        first, second = cut_of(chip_cols)
+        base, core = (row * 2 + col // 2) * chip_cols, col % 2
+        pieces = (lax.dynamic_slice_in_dim(start_block, base + core * (first // 2), first // 2), lax.dynamic_slice_in_dim(start_block, base + first + core * (second // 2), second // 2))
+        low_rows = jnp.concatenate(pieces).astype(jnp.bfloat16)
         for _ in range(SWEEPS):
-            projected = jnp.dot(data_local, basis_low, preferred_element_type=jnp.float32).astype(jnp.bfloat16)
-            pulled_part = lax.dot_general(data_local, projected, ROW_CONTRACT, preferred_element_type=jnp.float32)
-            pulled_rows = lax.psum_scatter(pulled_part, GROUP_AXES, scatter_dimension=0, tiled=True)
-            q_rows, basis_blocks = orthonormalize(pulled_rows)
-            basis_low = basis_blocks.reshape(start_block.shape)
-        q_basis = lax.all_gather(q_rows, GROUP_AXES, axis=0, tiled=True)
-        final_proj = jnp.dot(data_local, basis_low, preferred_element_type=jnp.float32)
-        ritz_vals = lax.psum(jnp.sum(final_proj * final_proj, axis=0), GROUP_AXES)
-        return q_basis, ritz_vals
+            q_rows, low_rows = orthonormalize(pull_rows(data_local, low_rows))
+        q_basis, ritz_vals = ritz(data_local, q_rows)
+        return q_basis, ritz_vals.reshape(-1)
 
     return jax.shard_map(device_sweeps, mesh=mesh, in_specs=(P(("batch", "row", "col"), None), P("batch", None)), out_specs=(P("batch", None), P("batch")), check_vma=False)

time: 1020 us -> 716 us (0.70)
  matrix products: 460 us -> 0 us
  Pallas kernels: 276 us -> 696 us
  waiting for transfers between devices: 235 us -> 0 us
  blocking collectives: 22.2 us -> 0 us
  between operations: 14.3 us -> 1.19 us
    pallas_call x0 -> x5, Pallas kernels: none -> 503 us  [the longest x4 438 us: pull_rows(): pl.pallas_call(pull_kernel, out_shape=jax.ShapeDtypeStruct((width, featur...]
    dot_general x9 -> x0, matrix products: 460 us -> none  [the longest x4 233 us: device_sweeps(): lax.dot_general(data_local, projected, ROW_CONTRACT, preferred_element_ty...]
    reduce_scatter x4 -> x0, waiting for transfers between devices: 235 us -> none  [device_sweeps(): lax.psum_scatter(pulled_part, GROUP_AXES, scatter_dimension=0, tiled=True)]
    pallas_call x4, Pallas kernels: 276 us -> 193 us  [orthonormalize(): pl.pallas_call(qr_kernel, out_shape=(jax.ShapeDtypeStruct((rows, width),...]
    psum x1 -> x0, blocking collectives: 22.2 us -> none  [device_sweeps(): ritz_vals = lax.psum(jnp.sum(final_proj * final_proj, axis=0), GROUP_AXES)]
  transfers between devices with their start and end apart: 5 -> 0, of which waited for: 4 -> 0; matrix products, arithmetic and copies ran while one was open for 4% -> 0% of each run, Pallas kernels for 0% -> 0%
where the time goes in v3:
time: 716 us; the launch traced here: 707 us
  Pallas kernels  696 us (97%)
  local copies, waits for them, and re-layouts  9.27 us (1%)
    pallas_call x4, Pallas kernels, pull_rows(): pl.pallas_call(pull_kernel, out_shape=jax.ShapeDtypeStruct((width, featur...  438 us
    pallas_call x4, Pallas kernels, orthonormalize(): pl.pallas_call(qr_kernel, out_shape=(jax.ShapeDtypeStruct((rows, width),...  193 us
    pallas_call x1, Pallas kernels, ritz(): pl.pallas_call(ritz_kernel, out_shape=(jax.ShapeDtypeStruct((features, wi...  64.6 us

profile of v3, /device:TPU:0, one launch (start us, length us, event | category | flops | bytes accessed | tf_op | source)
XLA Modules:
  0.0 707.2 jit_solution(15811278007626358545)
XLA Ops:
  0.7 1.0 dynamic-slice_convert_fusion.1
  1.7 1.1 dynamic-slice_convert_fusion
  2.8 0.8 pad_maximum_fusion.own
  3.6 111.4 %pull_rows.4.z_ref = f32[256,896]{1,0:T(8,128)} custom-call(bf16[8192,7168]{1,0:T(8,128)(2,1)} %data.9, bf16[896,256]{1,0:T(8,128)(2,1)} %pad_maximum_fusion.own), custom_call_target="tpu_custom_call" | custom-call | flops 60129542144 | bytes 234881024 | tf_op jit(solution)/shard_map/pull_rows/pallas_call | solution.py:384
  115.0 48.4 %orthonormalize.4 = (f32[896,256]{1,0:T(8,128)}, bf16[896,256]{1,0:T(8,128)(2,1)}) custom-call(f32[256,896]{1,0:T(8,128)} %pull_rows.4.z_ref), custom_call_target="tpu_custom_call" | custom-call | flops 4000000000 | bytes 6000000 | tf_op jit(solution)/shard_map/orthonormalize/pallas_call | solution.py:509
  163.3 109.0 %pull_rows.5.z_ref = f32[256,896]{1,0:T(8,128)} custom-call(bf16[8192,7168]{1,0:T(8,128)(2,1)} %data.9, bf16[896,256]{1,0:T(8,128)(2,1)} %get-tuple-element.8.own), custom_call_target="tpu_custom_call" | custom-call | flops 60129542144 | bytes 234881024 | tf_op jit(solution)/shard_map/pull_rows/pallas_call | solution.py:384
  272.4 48.2 %orthonormalize.5 = (f32[896,256]{1,0:T(8,128)}, bf16[896,256]{1,0:T(8,128)(2,1)}) custom-call(f32[256,896]{1,0:T(8,128)} %pull_rows.5.z_ref), custom_call_target="tpu_custom_call" | custom-call | flops 4000000000 | bytes 6000000 | tf_op jit(solution)/shard_map/orthonormalize/pallas_call | solution.py:509
  320.5 108.7 %pull_rows.6.z_ref = f32[256,896]{1,0:T(8,128)} custom-call(bf16[8192,7168]{1,0:T(8,128)(2,1)} %data.9, bf16[896,256]{1,0:T(8,128)(2,1)} %get-tuple-element.9.own), custom_call_target="tpu_custom_call" | custom-call | flops 60129542144 | bytes 234881024 | tf_op jit(solution)/shard_map/pull_rows/pallas_call | solution.py:384
  429.3 48.4 %orthonormalize.6 = (f32[896,256]{1,0:T(8,128)}, bf16[896,256]{1,0:T(8,128)(2,1)}) custom-call(f32[256,896]{1,0:T(8,128)} %pull_rows.6.z_ref), custom_call_target="tpu_custom_call" | custom-call | flops 4000000000 | bytes 6000000 | tf_op jit(solution)/shard_map/orthonormalize/pallas_call | solution.py:509
  477.7 108.9 %pull_rows.7.z_ref = f32[256,896]{1,0:T(8,128)} custom-call(bf16[8192,7168]{1,0:T(8,128)(2,1)} %data.9, bf16[896,256]{1,0:T(8,128)(2,1)} %get-tuple-element.10.own), custom_call_target="tpu_custom_call" | custom-call | flops 60129542144 | bytes 234881024 | tf_op jit(solution)/shard_map/pull_rows/pallas_call | solution.py:384
  586.6 48.4 %orthonormalize.7 = (f32[896,256]{1,0:T(8,128)}, bf16[896,256]{1,0:T(8,128)(2,1)}) custom-call(f32[256,896]{1,0:T(8,128)} %pull_rows.7.z_ref), custom_call_target="tpu_custom_call" | custom-call | flops 4000000000 | bytes 6000000 | tf_op jit(solution)/shard_map/orthonormalize/pallas_call | solution.py:509
  635.0 64.6 %ritz.1 = (f32[7168,256]{1,0:T(8,128)}, f32[1,256]{1,0:T(1,128)}) custom-call(bf16[8192,7168]{1,0:T(8,128)(2,1)} %data.9, f32[896,256]{1,0:T(8,128)} %get-tuple-element.11.own), custom_call_target="tpu_custom_call" | custom-call | flops 30064771072 | bytes 117440512 | tf_op jit(solution)/shard_map/ritz/pallas_call | solution.py:408
  699.6 0.0 copy-start
  699.6 6.6 copy.6
  706.2 0.0 copy-done
  706.2 0.6 copy.7
Async XLA Ops:
  699.6 6.6 copy-start

commit v4 on v3

--- a/solution.py
+++ b/solution.py
@@ -13,8 +13,10 @@
 HALF = 128
 PEERS = 7
 VMEM_BYTES = 63 * 1024 * 1024
-TILES = 8
-DEPTH = 8
+TILES = 2
+DEPTH = 3
+TURNS = 8 * TILES
+ROWS_AT_ONCE = 512
 
 
 def exact_dot(left, right, dims):
@@ -150,8 +152,8 @@
     by_width(sub, act)
 
 
-def first_pass(place, data, own, landing, basis, ring, acc, ring_sem, gather_sem, clear, finish, after):
-    turns = 8 * TILES
+def first_pass(place, data, own, landing, basis, ring, acc, ring_sem, gather_sem, second, clear, finish, after):
+    turns = TURNS
     tile_rows = ring.shape[1]
     for turn in range(DEPTH):
         tile_copy(place, data, ring, ring_sem, turn, turn, first_order, True)
@@ -202,7 +204,7 @@
         at(turn, 2 * TILES, (1,), (10,))
         at(turn, 2 * TILES, (7,), ())
         at(turn, 3 * TILES, (10,), ())
-        at(turn, 3 * TILES + 4, (3, 4), (8, 9, 11))
+        at(turn, 3 * TILES + TILES // 2, (3, 4), (8, 9, 11))
         at(turn, 4 * TILES, (8,), ())
         at(turn, 5 * TILES, (11,), ())
         at(turn, 6 * TILES - 1, (9, 6), (13, 12))
@@ -211,7 +213,7 @@
         slot = lax.rem(turn, DEPTH)
         flip_x, flip_y, sub = first_order(turn // TILES)
         tile_copy(place, data, ring, ring_sem, turn, slot, first_order, False)
-        part_rows = tile_rows // 2
+        part_rows = min(ROWS_AT_ONCE, tile_rows)
 
         def project(static):
             cols = place.columns(flip_x, flip_y, static)
@@ -219,7 +221,7 @@
                 @pl.when(lax.rem(turn, TILES) == 0)
                 def _():
                     basis[cols, :] = landing[cols, :].astype(jnp.bfloat16)
-            for half in range(2):
+            for half in range(tile_rows // part_rows):
                 inner = pl.ds(half * part_rows, part_rows)
                 rows = pl.ds(pl.multiple_of(lax.rem(turn, TILES) * tile_rows + half * part_rows, part_rows), part_rows)
                 acc[rows, :] += jnp.dot(ring[slot, inner, pl.ds(0, place.widths[static])], basis[cols, :], preferred_element_type=jnp.float32)
@@ -229,6 +231,11 @@
         @pl.when(turn + DEPTH < turns)
         def _():
             tile_copy(place, data, ring, ring_sem, turn + DEPTH, slot, first_order, True)
+
+        if second is not None:
+            @pl.when((turn + DEPTH >= turns) & (turn < turns - TILES))
+            def _():
+                tile_copy(place, data, ring, ring_sem, turn + DEPTH - (turns - TILES), slot, second, True)
 
         @pl.when(turn >= turns - TILES)
         def _():
@@ -247,7 +254,7 @@
     halves = tuple(width // 2 for width in place.widths)
     width = z_ref.shape[0]
     top = width // 2
-    turns = 8 * TILES
+    turns = TURNS
 
     def clear():
         part0[...] = jnp.zeros_like(part0)
@@ -256,7 +263,7 @@
     def finish(tile, rows):
         proj_t[tile] = rows.astype(jnp.bfloat16).T
 
-    first_pass(place, data, own, basis, basis, ring, acc, ring_sem, gather_sem, clear, finish, lambda: None)
+    first_pass(place, data, own, basis, basis, ring, acc, ring_sem, gather_sem, second_order, clear, finish, lambda: None)
 
     upper, lower = pl.ds(0, top), pl.ds(top, width - top)
     mine = tuple(pl.ds(pl.multiple_of(place.core * half, HALF), half) for half in halves)
@@ -297,11 +304,11 @@
 
     @pl.loop(0, turns)
     def _(turn):
-        slot = lax.rem(turn, DEPTH)
+        slot = lax.rem(turn + turns - TILES, DEPTH)
         block, tile = turn // TILES, lax.rem(turn, TILES)
         sub = second_order(block)[2]
 
-        @pl.when(turn >= DEPTH)
+        @pl.when(turn >= TILES)
         def _():
             tile_copy(place, data, ring, ring_sem, turn, slot, second_order, False)
 
@@ -319,9 +326,9 @@
         for index, (held, held_sub) in enumerate(order):
             pl.when(turn == (index + 1) * TILES - 1)(lambda held=held, held_sub=held_sub: swaps[held, held_sub].start())
             if held == FAR:
-                pl.when(turn == (index + 1) * TILES + 2)(lambda held_sub=held_sub: send_far(held_sub))
+                pl.when(turn == (index + 1) * TILES + 0)(lambda held_sub=held_sub: send_far(held_sub))
             elif held != OWN:
-                pl.when(turn == (index + 1) * TILES + 3)(lambda held=held, held_sub=held_sub: send_side(held, held_sub))
+                pl.when(turn == (index + 1) * TILES + 0)(lambda held=held, held_sub=held_sub: send_side(held, held_sub))
 
     for sub in range(2):
         lanes = pl.ds(sub * halves[0], halves[sub])
@@ -362,7 +369,7 @@
             total = total + slots[index]
         r_ref[...] = jnp.sum(total, axis=0, keepdims=True)
 
-    first_pass(place, data, own, q_ref, basis, ring, acc, ring_sem, gather_sem, clear, finish, after)
+    first_pass(place, data, own, q_ref, basis, ring, acc, ring_sem, gather_sem, None, clear, finish, after)
 
 
 def stream_scratch(rows, features, width):
@@ -485,10 +492,14 @@
         share_gram(turn)
         factor_inverse(gram.at[turn], work, inv_low)
 
-        @pl.loop(0, rows // HALF)
+        @pl.loop(0, rows // (2 * HALF))
         def _(i):
-            block = pl.ds(pl.multiple_of(i * HALF, HALF), HALF)
+            block = pl.ds(pl.multiple_of(i * 2 * HALF, 2 * HALF), 2 * HALF)
             turned[:, block] = exact_dot(inv_low[...], turned[:, block], PLAIN)
+
+        if rows % (2 * HALF):
+            rest = pl.ds(rows // (2 * HALF) * 2 * HALF, HALF)
+            turned[:, rest] = exact_dot(inv_low[...], turned[:, rest], PLAIN)
 
         @pl.when(turn == 0)
         def _():

time: 716 us -> 639 us (0.89)
  Pallas kernels: 696 us -> 620 us
    pallas_call x4, Pallas kernels: 438 us -> 379 us  [pull_rows(): pl.pallas_call(pull_kernel, out_shape=jax.ShapeDtypeStruct((width, featur...]
    pallas_call x4, Pallas kernels: 193 us -> 183 us  [orthonormalize(): pl.pallas_call(qr_kernel, out_shape=(jax.ShapeDtypeStruct((rows, width),...]
where the time goes in v4:
time: 639 us; the launch traced here: 631 us
  Pallas kernels  620 us (97%)
  local copies, waits for them, and re-layouts  9.27 us (1%)
    pallas_call x4, Pallas kernels, pull_rows(): pl.pallas_call(pull_kernel, out_shape=jax.ShapeDtypeStruct((width, featur...  379 us
    pallas_call x4, Pallas kernels, orthonormalize(): pl.pallas_call(qr_kernel, out_shape=(jax.ShapeDtypeStruct((rows, width),...  183 us
    pallas_call x1, Pallas kernels, ritz(): pl.pallas_call(ritz_kernel, out_shape=(jax.ShapeDtypeStruct((features, wi...  57.9 us

profile of v4, /device:TPU:0, one launch (start us, length us, event | category | flops | bytes accessed | tf_op | source)
XLA Modules:
  0.0 631.1 jit_solution(3956954543906745197)
XLA Ops:
  0.7 1.0 dynamic-slice_convert_fusion.1
  1.7 1.1 dynamic-slice_convert_fusion
  2.8 0.8 pad_maximum_fusion.own
  3.6 96.0 %pull_rows.4.z_ref = f32[256,896]{1,0:T(8,128)} custom-call(bf16[8192,7168]{1,0:T(8,128)(2,1)} %data.9, bf16[896,256]{1,0:T(8,128)(2,1)} %pad_maximum_fusion.own), custom_call_target="tpu_custom_call" | custom-call | flops 60129542144 | bytes 234881024 | tf_op jit(solution)/shard_map/pull_rows/pallas_call | solution.py:391
  99.6 46.3 %orthonormalize.4 = (f32[896,256]{1,0:T(8,128)}, bf16[896,256]{1,0:T(8,128)(2,1)}) custom-call(f32[256,896]{1,0:T(8,128)} %pull_rows.4.z_ref), custom_call_target="tpu_custom_call" | custom-call | flops 4000000000 | bytes 6000000 | tf_op jit(solution)/shard_map/orthonormalize/pallas_call | solution.py:520
  145.9 94.3 %pull_rows.5.z_ref = f32[256,896]{1,0:T(8,128)} custom-call(bf16[8192,7168]{1,0:T(8,128)(2,1)} %data.9, bf16[896,256]{1,0:T(8,128)(2,1)} %get-tuple-element.8.own), custom_call_target="tpu_custom_call" | custom-call | flops 60129542144 | bytes 234881024 | tf_op jit(solution)/shard_map/pull_rows/pallas_call | solution.py:391
  240.2 45.6 %orthonormalize.5 = (f32[896,256]{1,0:T(8,128)}, bf16[896,256]{1,0:T(8,128)(2,1)}) custom-call(f32[256,896]{1,0:T(8,128)} %pull_rows.5.z_ref), custom_call_target="tpu_custom_call" | custom-call | flops 4000000000 | bytes 6000000 | tf_op jit(solution)/shard_map/orthonormalize/pallas_call | solution.py:520
  285.8 94.1 %pull_rows.6.z_ref = f32[256,896]{1,0:T(8,128)} custom-call(bf16[8192,7168]{1,0:T(8,128)(2,1)} %data.9, bf16[896,256]{1,0:T(8,128)(2,1)} %get-tuple-element.9.own), custom_call_target="tpu_custom_call" | custom-call | flops 60129542144 | bytes 234881024 | tf_op jit(solution)/shard_map/pull_rows/pallas_call | solution.py:391
  379.9 45.7 %orthonormalize.6 = (f32[896,256]{1,0:T(8,128)}, bf16[896,256]{1,0:T(8,128)(2,1)}) custom-call(f32[256,896]{1,0:T(8,128)} %pull_rows.6.z_ref), custom_call_target="tpu_custom_call" | custom-call | flops 4000000000 | bytes 6000000 | tf_op jit(solution)/shard_map/orthonormalize/pallas_call | solution.py:520
  425.7 94.3 %pull_rows.7.z_ref = f32[256,896]{1,0:T(8,128)} custom-call(bf16[8192,7168]{1,0:T(8,128)(2,1)} %data.9, bf16[896,256]{1,0:T(8,128)(2,1)} %get-tuple-element.10.own), custom_call_target="tpu_custom_call" | custom-call | flops 60129542144 | bytes 234881024 | tf_op jit(solution)/shard_map/pull_rows/pallas_call | solution.py:391
  520.0 45.6 %orthonormalize.7 = (f32[896,256]{1,0:T(8,128)}, bf16[896,256]{1,0:T(8,128)(2,1)}) custom-call(f32[256,896]{1,0:T(8,128)} %pull_rows.7.z_ref), custom_call_target="tpu_custom_call" | custom-call | flops 4000000000 | bytes 6000000 | tf_op jit(solution)/shard_map/orthonormalize/pallas_call | solution.py:520
  565.6 57.9 %ritz.1 = (f32[7168,256]{1,0:T(8,128)}, f32[1,256]{1,0:T(1,128)}) custom-call(bf16[8192,7168]{1,0:T(8,128)(2,1)} %data.9, f32[896,256]{1,0:T(8,128)} %get-tuple-element.11.own), custom_call_target="tpu_custom_call" | custom-call | flops 30064771072 | bytes 117440512 | tf_op jit(solution)/shard_map/ritz/pallas_call | solution.py:415
  623.4 0.0 copy-start
  623.4 6.6 %copy.6 = f32[7168,256]{1,0:T(8,128)} copy(f32[7168,256]{1,0:T(8,128)} %get-tuple-element.16) | data formatting | bytes 14680064
  630.1 0.0 copy-done
  630.1 0.6 copy.7
Async XLA Ops:
  623.4 6.6 %copy-start = (f32[1,256]{1,0:T(1,128)S(1)}, f32[1,256]{1,0:T(1,128)}, u32[]{:S(2)}) copy-start(f32[1,256]{1,0:T(1,128)} %get-tuple-element.13) | copy-start | bytes 3076

commit v5 on v4

v5 whole, which is shorter than its diff:
```python
import jax
import jax.numpy as jnp
from jax import lax
from jax.experimental import pallas as pl
from jax.experimental.pallas import tpu as pltpu
from jax.sharding import PartitionSpec as P

SWEEPS = 4
ROW_CONTRACT = (((0,), (0,)), ((), ()))
LANE_CONTRACT = (((1,), (1,)), ((), ()))
PLAIN = (((1,), (0,)), ((), ()))
MESH = pl.DeviceIdType.MESH
HALF = 128
PEERS = 7
VMEM_BYTES = 63 * 1024 * 1024
TILES = 2
DEPTH = 3
TURNS = 8 * TILES
ROWS_AT_ONCE = 512


def exact_dot(left, right, dims):
    return lax.dot_general(left, right, dims, precision=lax.Precision.HIGHEST, preferred_element_type=jnp.float32)


def invert_factor(block):
    lane = lax.broadcasted_iota(jnp.int32, (8, HALF), 1)
    sub = lax.broadcasted_iota(jnp.int32, (8, HALF), 0)
    for step in range(HALF // 8):
        base = 8 * step
        inside = (lane >= base) & (lane < base + 8)
        pivots = block[base:base + 8, :]
        cols = [jnp.broadcast_to(pivots[:, base + p:base + p + 1], (8, HALF)) for p in range(8)]
        low = jnp.where(inside, jnp.where(lane - base == sub, 1.0, 0.0), pivots)
        full = low
        scale = jnp.zeros((8, HALF), jnp.float32)
        inverse = jnp.zeros((8, HALF), jnp.float32)
        for p in range(8):
            root = lax.rsqrt(jnp.broadcast_to(cols[p][p:p + 1, :], (8, HALF)))
            recip = root * root
            here = sub == p
            scale = jnp.where(here, root, scale)
            inverse = jnp.where(here, recip, inverse)
            mult = jnp.where(here, 0.0, cols[p] * recip)
            for q in range(p + 1, 8):
                cols[q] = cols[q] - mult * jnp.broadcast_to(cols[q][p:p + 1, :], (8, HALF))
            full_row = jnp.broadcast_to(full[p:p + 1, :], (8, HALF))
            low_row = jnp.broadcast_to(low[p:p + 1, :], (8, HALF))
            full = full - mult * full_row
            low = low - jnp.where(sub > p, mult, 0.0) * low_row
        block[base:base + 8, :] = low * scale
        full = full * inverse
        rows = [jnp.broadcast_to(full[p:p + 1, :], (8, HALF)) for p in range(8)]
        for i in range(step + 1, HALF // 8):
            held = block[8 * i:8 * i + 8, :]
            acc = jnp.where(inside, 0.0, held)
            for p in range(8):
                acc = acc - jnp.broadcast_to(held[:, base + p:base + p + 1], (8, HALF)) * rows[p]
            block[8 * i:8 * i + 8, :] = acc


def factor_inverse(gram, work, inv_low):
    tri = lax.broadcasted_iota(jnp.int32, (HALF, HALF), 0) >= lax.broadcasted_iota(jnp.int32, (HALF, HALF), 1)
    inv_low[:HALF, HALF:] = jnp.zeros((HALF, HALF), jnp.float32)

    @pl.loop(0, 2)
    def _(half):
        @pl.when(half == 0)
        def _():
            work[...] = gram[0:HALF, :]

        @pl.when(half == 1)
        def _():
            upper = exact_dot(inv_low[:HALF, :HALF], gram[HALF:2 * HALF, :], PLAIN)
            work[...] = gram[2 * HALF:3 * HALF, :] - exact_dot(upper, upper, ROW_CONTRACT)
            inv_low[HALF:, :HALF] = exact_dot(upper, inv_low[:HALF, :HALF], ROW_CONTRACT)

        invert_factor(work)
        block_inv = jnp.where(tri, work[...], 0.0)

        @pl.when(half == 0)
        def _():
            inv_low[:HALF, :HALF] = block_inv

        @pl.when(half == 1)
        def _():
            inv_low[HALF:, HALF:] = block_inv
            inv_low[HALF:, :HALF] = -exact_dot(block_inv, inv_low[HALF:, :HALF], PLAIN)


def orthonormalize(q_ref, low_ref, turned, part, slots, gram, work, inv_low, sum_send, sum_recv, out_send, out_recv):
    row, col = lax.axis_index("row"), lax.axis_index("col")
    me = row * 4 + col
    chunk = 3 * HALF // 8
    rows = turned.shape[1]

    def peer(offset):
        other = lax.rem(me + offset, 8)
        return (0, other // 4, lax.rem(other, 4)), other

    def share_gram(turn):
        mine = pl.ds(pl.multiple_of(me * chunk, 8), chunk)
        copies = []
        for offset in range(1, 8):
            device, other = peer(offset)
            copy = pltpu.make_async_remote_copy(
                src_ref=part.at[turn, pl.ds(pl.multiple_of(other * chunk, 8), chunk)],
                dst_ref=slots.at[turn, offset - 1],
                send_sem=sum_send.at[turn, offset - 1],
                recv_sem=sum_recv.at[turn, offset - 1],
                device_id=device,
                device_id_type=MESH,
            )
            copy.start()
            copies.append(copy)
        total = part[turn, mine, :]
        for offset in range(1, 8):
            copies[offset - 1].wait_recv()
            total = total + slots[turn, offset - 1]
        gram[turn, mine, :] = total
        spread = []
        for offset in range(1, 8):
            copy = pltpu.make_async_remote_copy(
                src_ref=gram.at[turn, mine],
                dst_ref=gram.at[turn, mine],
                send_sem=out_send.at[turn, offset - 1],
                recv_sem=out_recv.at[turn, offset - 1],
                device_id=peer(offset)[0],
                device_id_type=MESH,
            )
            copy.start()
            spread.append(copy)
        for copy in copies:
            copy.wait_send()
        for copy in spread:
            copy.wait()

    z_left, z_right = turned[:HALF, :].astype(jnp.bfloat16), turned[HALF:, :].astype(jnp.bfloat16)
    for place, (left, right) in enumerate(((z_left, z_left), (z_left, z_right), (z_right, z_right))):
        part[0, HALF * place:HALF * (place + 1), :] = lax.dot_general(left, right, LANE_CONTRACT, preferred_element_type=jnp.float32)

    def turn_body(turn):
        share_gram(turn)
        factor_inverse(gram.at[turn], work, inv_low)

        @pl.loop(0, rows // (2 * HALF))
        def _(i):
            block = pl.ds(pl.multiple_of(i * 2 * HALF, 2 * HALF), 2 * HALF)
            turned[:, block] = exact_dot(inv_low[...], turned[:, block], PLAIN)

        if rows % (2 * HALF):
            rest = pl.ds(rows // (2 * HALF) * 2 * HALF, HALF)
            turned[:, rest] = exact_dot(inv_low[...], turned[:, rest], PLAIN)

        @pl.when(turn == 0)
        def _():
            for place, (left, right) in enumerate(((0, 0), (0, HALF), (HALF, HALF))):
                part[1, HALF * place:HALF * (place + 1), :] = exact_dot(turned[left:left + HALF, :], turned[right:right + HALF, :], LANE_CONTRACT)

    pl.loop(0, 2)(turn_body)

    @pl.loop(0, rows // HALF)
    def _(i):
        block = pl.ds(pl.multiple_of(i * HALF, HALF), HALF)
        q_ref[block, :] = turned[:, block].T
        low_ref[block, :] = q_ref[block, :].astype(jnp.bfloat16)


def cut_of(chip_cols):
    first = 2 * HALF * ((chip_cols // (2 * HALF) + 1) // 2)
    return first, chip_cols - first


class Place:
    def __init__(self, features):
        self.row, self.col = lax.axis_index("row"), lax.axis_index("col")
        self.core, self.x = lax.rem(self.col, 2), self.col // 2
        self.twin = (0, self.row, self.col + 1 - 2 * self.core)
        self.x_side = (0, self.row, self.core + 2 * (1 - self.x))
        self.y_side = (0, 1 - self.row, self.col)
        self.chip_cols = features // 4
        self.widths = cut_of(self.chip_cols)

    def chip(self, flip_x, flip_y):
        x = self.x + flip_x - 2 * self.x * flip_x
        y = self.row + flip_y - 2 * self.row * flip_y
        return y * 2 + x

    def columns(self, flip_x, flip_y, sub):
        start = self.chip(flip_x, flip_y) * self.chip_cols + sub * self.widths[0]
        return pl.ds(pl.multiple_of(start, 2 * HALF), self.widths[sub])

    def owned(self, flip_x, flip_y, sub):
        start = self.chip(flip_x, flip_y) * self.chip_cols + sub * self.widths[0] + self.core * (self.widths[sub] // 2)
        return pl.ds(pl.multiple_of(start, HALF), self.widths[sub] // 2)


def as_int(flag):
    return jnp.where(flag, 1, 0)


def first_order(block):
    far = block >= 6
    in_x = (block == 2) | (block == 4) | far
    in_y = (block == 3) | (block == 5) | far
    return as_int(in_x), as_int(in_y), as_int((block == 1) | ((block >= 4) & (block <= 6)))


def second_order(block):
    far = block < 2
    in_x = far | (block == 3) | (block == 5)
    in_y = far | (block == 2) | (block == 4)
    return as_int(in_x), as_int(in_y), as_int((block == 1) | (block == 4) | (block == 5) | (block == 7))


def by_width(sub, action):
    for static in range(2):
        pl.when(sub == static)(lambda static=static: action(static))


def tile_copy(place, data, ring, ring_sem, tile, slot, order, begin):
    flip_x, flip_y, sub = order(tile // TILES)
    tile_rows = ring.shape[1]
    rows = pl.ds(pl.multiple_of(lax.rem(tile, TILES) * tile_rows, tile_rows), tile_rows)

    def act(static):
        copy = pltpu.make_async_copy(data.at[rows, place.columns(flip_x, flip_y, static)], ring.at[slot, :, pl.ds(0, place.widths[static])], ring_sem.at[slot])
        copy.start() if begin else copy.wait()

    by_width(sub, act)


def first_pass(place, data, own, landing, basis, ring, acc, ring_sem, gather_sem, second, clear, finish, after):
    turns = TURNS
    tile_rows = ring.shape[1]
    for turn in range(DEPTH):
        tile_copy(place, data, ring, ring_sem, turn, turn, first_order, True)

    barrier = pltpu.get_barrier_semaphore()
    for offset in range(1, 8):
        other = lax.rem(place.row * 4 + place.col + offset, 8)
        pl.semaphore_signal(barrier, inc=1, device_id=(0, other // 4, lax.rem(other, 4)), device_id_type=MESH)
    pl.semaphore_wait(barrier, PEERS)

    piece = (pl.ds(0, place.widths[0] // 2), pl.ds(place.widths[0] // 2, place.widths[1] // 2))

    def hand(index, flip_x, flip_y, sub, device):
        rows = place.owned(flip_x, flip_y, sub)
        source = own.at[piece[sub]] if flip_x + flip_y == 0 else landing.at[rows]
        return pltpu.make_async_remote_copy(
            src_ref=source, dst_ref=landing.at[rows], send_sem=gather_sem.at[0, index], recv_sem=gather_sem.at[1, index], device_id=device, device_id_type=MESH
        )

    twin, x_side, y_side = place.twin, place.x_side, place.y_side
    copies = [
        hand(0, 0, 0, 0, x_side), hand(1, 0, 0, 0, y_side), hand(2, 0, 0, 0, twin),
        hand(3, 0, 0, 1, x_side), hand(4, 0, 0, 1, y_side), hand(5, 0, 0, 1, twin),
        hand(6, 1, 0, 0, y_side), hand(7, 1, 0, 0, twin), hand(8, 1, 0, 1, twin),
        hand(9, 0, 1, 1, x_side), hand(10, 0, 1, 0, twin), hand(11, 0, 1, 1, twin),
        hand(12, 1, 1, 0, twin), hand(13, 1, 1, 1, twin),
    ]
    for index in range(6):
        copies[index].start()
    for sub in range(2):
        landing[place.owned(0, 0, sub), :] = own[piece[sub], :]
    acc[...] = jnp.zeros_like(acc)
    clear()

    def at(turn, when, waits, starts):
        @pl.when(turn == when)
        def _():
            for index in waits:
                copies[index].wait_recv()
            for index in starts:
                copies[index].start()

    @pl.loop(0, turns)
    def _(turn):
        at(turn, 0, (2,), ())
        at(turn, TILES, (5,), ())
        at(turn, 2 * TILES - 1, (0,), (6, 7))
        at(turn, 2 * TILES - 1, (1,), (10,))
        at(turn, 2 * TILES, (7,), ())
        at(turn, 3 * TILES, (10,), ())
        at(turn, 3 * TILES + TILES // 2, (3, 4), (8, 9, 11))
        at(turn, 4 * TILES, (8,), ())
        at(turn, 5 * TILES, (11,), ())
        at(turn, 6 * TILES - 1, (9, 6), (13, 12))
        at(turn, 6 * TILES, (13,), ())
        at(turn, 7 * TILES, (12,), ())
        slot = lax.rem(turn, DEPTH)
        flip_x, flip_y, sub = first_order(turn // TILES)
        tile_copy(place, data, ring, ring_sem, turn, slot, first_order, False)
        part_rows = min(ROWS_AT_ONCE, tile_rows)

        def project(static):
            cols = place.columns(flip_x, flip_y, static)
            if landing is not basis:
                @pl.when(lax.rem(turn, TILES) == 0)
                def _():
                    basis[cols, :] = landing[cols, :].astype(jnp.bfloat16)
            for half in range(tile_rows // part_rows):
                inner = pl.ds(half * part_rows, part_rows)
                rows = pl.ds(pl.multiple_of(lax.rem(turn, TILES) * tile_rows + half * part_rows, part_rows), part_rows)
                acc[rows, :] += jnp.dot(ring[slot, inner, pl.ds(0, place.widths[static])], basis[cols, :], preferred_element_type=jnp.float32)

        by_width(sub, project)

        @pl.when(turn + DEPTH < turns)
        def _():
            tile_copy(place, data, ring, ring_sem, turn + DEPTH, slot, first_order, True)

        if second is not None:
            @pl.when((turn + DEPTH >= turns) & (turn < turns - TILES))
            def _():
                tile_copy(place, data, ring, ring_sem, turn + DEPTH - (turns - TILES), slot, second, True)

        @pl.when(turn >= turns - TILES)
        def _():
            tile = lax.rem(turn, TILES)
            finish(tile, acc[pl.ds(pl.multiple_of(tile * tile_rows, tile_rows), tile_rows), :])

    after()
    for copy in copies:
        copy.wait_send()


def sweep_kernel(data, own, q_ref, low_ref, turned, gram_part, gram_slots, gram, work, inv_low, sum_send, sum_recv, out_send, out_recv, basis, ring, acc, proj_t, part0, part1, twin0, twin1, far0, far1, side0, side1, ring_sem, gather_sem, twin_sem, far_sem, side_sem):
    place = Place(data.shape[1])
    twin, x_side, y_side = place.twin, place.x_side, place.y_side
    part, from_twin, from_far, from_side = (part0, part1), (twin0, twin1), (far0, far1), (side0, side1)
    halves = tuple(width // 2 for width in place.widths)
    width = turned.shape[0]
    top = width // 2
    turns = TURNS

    def clear():
        part0[...] = jnp.zeros_like(part0)
        part1[...] = jnp.zeros_like(part1)

    def finish(tile, rows):
        proj_t[tile] = rows.astype(jnp.bfloat16).T

    first_pass(place, data, own, basis, basis, ring, acc, ring_sem, gather_sem, second_order, clear, finish, lambda: None)

    upper, lower = pl.ds(0, top), pl.ds(top, width - top)
    mine = tuple(pl.ds(pl.multiple_of(place.core * half, HALF), half) for half in halves)
    other = tuple(pl.ds(pl.multiple_of((1 - place.core) * half, HALF), half) for half in halves)
    FAR, Y, X, OWN = 0, 1, 2, 3

    def remote(source, target, sems, device):
        return pltpu.make_async_remote_copy(src_ref=source, dst_ref=target, send_sem=sems.at[0], recv_sem=sems.at[1], device_id=device, device_id_type=MESH)

    swaps, relays, delivers = {}, {}, {}
    for sub in range(2):
        for kind in range(4):
            swaps[kind, sub] = remote(part[sub].at[kind, :, other[sub]], from_twin[sub].at[kind], twin_sem.at[kind, sub], twin)
        relays[0, sub] = remote(part[sub].at[FAR, upper, mine[sub]], from_far[sub].at[0], far_sem.at[0, sub], x_side)
        relays[1, sub] = remote(part[sub].at[FAR, lower, mine[sub]], from_far[sub].at[1], far_sem.at[1, sub], y_side)
        for kind, device in ((Y, y_side), (X, x_side)):
            for which, rows in ((0, upper), (1, lower)):
                delivers[kind, which, sub] = remote(part[sub].at[kind, rows, mine[sub]], from_side[sub].at[kind - 1, rows], side_sem.at[kind - 1, which, sub], device)

    def lift(kind, sub):
        swaps[kind, sub].wait_recv()
        part[sub][kind, :, mine[sub]] = part[sub][kind, :, mine[sub]] + from_twin[sub][kind]

    def send_far(sub):
        lift(FAR, sub)
        relays[0, sub].start()
        relays[1, sub].start()

    def send_side(kind, sub):
        lift(kind, sub)
        plain, joined, rows = (1, 0, upper) if kind == Y else (0, 1, lower)
        delivers[kind, plain, sub].start()
        relays[joined, sub].wait_recv()
        part[sub][kind, rows, mine[sub]] = part[sub][kind, rows, mine[sub]] + from_far[sub][joined]
        delivers[kind, joined, sub].start()

    order = ((FAR, 0), (FAR, 1), (Y, 0), (X, 0), (Y, 1), (X, 1), (OWN, 0), (OWN, 1))

    @pl.loop(0, turns)
    def _(turn):
        slot = lax.rem(turn + turns - TILES, DEPTH)
        block, tile = turn // TILES, lax.rem(turn, TILES)
        sub = second_order(block)[2]

        @pl.when(turn >= TILES)
        def _():
            tile_copy(place, data, ring, ring_sem, turn, slot, second_order, False)

        kind = jnp.where(block < 2, FAR, jnp.where(block >= 6, OWN, jnp.where((block == 2) | (block == 4), Y, X)))

        def pull(static):
            part[static][kind] += jnp.dot(proj_t[tile], ring[slot, :, pl.ds(0, place.widths[static])], preferred_element_type=jnp.float32)

        by_width(sub, pull)

        @pl.when(turn + DEPTH < turns)
        def _():
            tile_copy(place, data, ring, ring_sem, turn + DEPTH, slot, second_order, True)

        for index, (held, held_sub) in enumerate(order):
            pl.when(turn == (index + 1) * TILES - 1)(lambda held=held, held_sub=held_sub: swaps[held, held_sub].start())
            if held == FAR:
                pl.when(turn == (index + 1) * TILES + 0)(lambda held_sub=held_sub: send_far(held_sub))
            elif held != OWN:
                pl.when(turn == (index + 1) * TILES + 0)(lambda held=held, held_sub=held_sub: send_side(held, held_sub))

    for sub in range(2):
        lanes = pl.ds(sub * halves[0], halves[sub])
        lift(OWN, sub)
        for kind in (Y, X):
            for which in range(2):
                delivers[kind, which, sub].wait_recv()
        turned[:, lanes] = (part[sub][OWN, :, mine[sub]] + from_side[sub][0]) + from_side[sub][1]
    orthonormalize(q_ref, low_ref, turned, gram_part, gram_slots, gram, work, inv_low, sum_send, sum_recv, out_send, out_recv)
    for copy in (*swaps.values(), *relays.values(), *delivers.values()):
        copy.wait_send()


def ritz_kernel(data, own, q_ref, r_ref, basis, ring, acc, slots, ring_sem, gather_sem, share_sem):
    place = Place(data.shape[1])
    me = place.row * 4 + place.col
    width = q_ref.shape[1]

    def clear():
        slots[me] = jnp.zeros((8, width), jnp.float32)

    def finish(tile, rows):
        slots[me] += jnp.sum((rows * rows).reshape(rows.shape[0] // 8, 8, width), axis=0)

    def after():
        sends = []
        for offset in range(1, 8):
            other = lax.rem(me + offset, 8)
            copy = pltpu.make_async_remote_copy(
                src_ref=slots.at[me], dst_ref=slots.at[me], send_sem=share_sem.at[0, offset - 1], recv_sem=share_sem.at[1, offset - 1],
                device_id=(0, other // 4, lax.rem(other, 4)), device_id_type=MESH,
            )
            copy.start()
            sends.append(copy)
        for copy in sends:
            copy.wait()
        total = slots[0]
        for index in range(1, 8):
            total = total + slots[index]
        r_ref[...] = jnp.sum(total, axis=0, keepdims=True)

    first_pass(place, data, own, q_ref, basis, ring, acc, ring_sem, gather_sem, None, clear, finish, after)


def stream_scratch(rows, features, width):
    return [
        pltpu.VMEM((features, width), jnp.bfloat16),
        pltpu.VMEM((DEPTH, rows // TILES, cut_of(features // 4)[0]), jnp.bfloat16),
        pltpu.VMEM((rows, width), jnp.float32),
    ]


def sweep(data_local, own):
    rows, features = data_local.shape
    width = own.shape[1]
    widths = cut_of(features // 4)
    pairs = []
    for shape in ((4, width), (4, width), (2, width // 2), (2, width)):
        scale = 1 if not pairs else 2
        pairs += [pltpu.VMEM((*shape, size // scale), jnp.float32) for size in widths]
    return pl.pallas_call(
        sweep_kernel,
        out_shape=(jax.ShapeDtypeStruct((features // 8, width), jnp.float32), jax.ShapeDtypeStruct((features // 8, width), jnp.bfloat16)),
        in_specs=[pl.BlockSpec(memory_space=pl.ANY), pl.BlockSpec(memory_space=pltpu.VMEM)],
        out_specs=(pl.BlockSpec(memory_space=pltpu.VMEM), pl.BlockSpec(memory_space=pltpu.VMEM)),
        scratch_shapes=[
            pltpu.VMEM((width, features // 8), jnp.float32),
            pltpu.VMEM((2, 3 * HALF, HALF), jnp.float32),
            pltpu.VMEM((2, PEERS, 3 * HALF // 8, HALF), jnp.float32),
            pltpu.VMEM((2, 3 * HALF, HALF), jnp.float32),
            pltpu.VMEM((HALF, HALF), jnp.float32),
            pltpu.VMEM((2 * HALF, 2 * HALF), jnp.float32),
            pltpu.SemaphoreType.DMA((2, PEERS)),
            pltpu.SemaphoreType.DMA((2, PEERS)),
            pltpu.SemaphoreType.DMA((2, PEERS)),
            pltpu.SemaphoreType.DMA((2, PEERS)),
            *stream_scratch(rows, features, width),
            pltpu.VMEM((TILES, width, rows // TILES), jnp.bfloat16),
            *pairs,
            pltpu.SemaphoreType.DMA((DEPTH,)),
            pltpu.SemaphoreType.DMA((2, 14)),
            pltpu.SemaphoreType.DMA((4, 2, 2)),
            pltpu.SemaphoreType.DMA((2, 2, 2)),
            pltpu.SemaphoreType.DMA((2, 2, 2, 2)),
        ],
        compiler_params=pltpu.CompilerParams(collective_id=1, has_side_effects=True, vmem_limit_bytes=VMEM_BYTES),
        cost_estimate=pl.CostEstimate(flops=4 * rows * features * width, bytes_accessed=4 * rows * features, transcendentals=0),
        name="sweep",
    )(data_local, own)


def ritz(data_local, own):
    rows, features = data_local.shape
    width = own.shape[1]
    return pl.pallas_call(
        ritz_kernel,
        out_shape=(jax.ShapeDtypeStruct((features, width), jnp.float32), jax.ShapeDtypeStruct((1, width), jnp.float32)),
        in_specs=[pl.BlockSpec(memory_space=pl.ANY), pl.BlockSpec(memory_space=pltpu.VMEM)],
        out_specs=(pl.BlockSpec(memory_space=pltpu.VMEM), pl.BlockSpec(memory_space=pltpu.VMEM)),
        scratch_shapes=[
            *stream_scratch(rows, features, width),
            pltpu.VMEM((8, 8, width), jnp.float32),
            pltpu.SemaphoreType.DMA((DEPTH,)),
            pltpu.SemaphoreType.DMA((2, 14)),
            pltpu.SemaphoreType.DMA((2, 7)),
        ],
        compiler_params=pltpu.CompilerParams(collective_id=2, has_side_effects=True, vmem_limit_bytes=VMEM_BYTES),
        cost_estimate=pl.CostEstimate(flops=2 * rows * features * width, bytes_accessed=2 * rows * features, transcendentals=0),
        name="ritz",
    )(data_local, own)


def solution(mesh):
    def device_sweeps(data_local, start_block):
        chip_cols = start_block.shape[0] // 4
        row, col = lax.axis_index("row"), lax.axis_index("col")
        first, second = cut_of(chip_cols)
        base, core = (row * 2 + col // 2) * chip_cols, col % 2
        pieces = (lax.dynamic_slice_in_dim(start_block, base + core * (first // 2), first // 2), lax.dynamic_slice_in_dim(start_block, base + first + core * (second // 2), second // 2))
        low_rows = jnp.concatenate(pieces).astype(jnp.bfloat16)
        for _ in range(SWEEPS):
            q_rows, low_rows = sweep(data_local, low_rows)
        q_basis, ritz_vals = ritz(data_local, q_rows)
        return q_basis, ritz_vals.reshape(-1)

    return jax.shard_map(device_sweeps, mesh=mesh, in_specs=(P(("batch", "row", "col"), None), P("batch", None)), out_specs=(P("batch", None), P("batch")), check_vma=False)
```

time: 639 us -> 618 us (0.967)
  Pallas kernels: 620 us -> 599 us
    pallas_call x8 -> x4, Pallas kernels: 562 us -> 541 us  [sweep(): pl.pallas_call(sweep_kernel, out_shape=(jax.ShapeDtypeStruct((features //...]
where the time goes in v5:
time: 618 us; the launch traced here: 611 us
  Pallas kernels  599 us (97%)
  local copies, waits for them, and re-layouts  9.27 us (2%)
    pallas_call x4, Pallas kernels, sweep(): pl.pallas_call(sweep_kernel, out_shape=(jax.ShapeDtypeStruct((features //...  541 us
    pallas_call x1, Pallas kernels, ritz(): pl.pallas_call(ritz_kernel, out_shape=(jax.ShapeDtypeStruct((features, wi...  58.7 us

profile of v5, /device:TPU:0, one launch (start us, length us, event | category | flops | bytes accessed | tf_op | source)
XLA Modules:
  0.0 610.5 jit_solution(12829276124985015842)
XLA Ops:
  0.7 1.0 dynamic-slice_convert_fusion.1
  1.7 1.1 dynamic-slice_convert_fusion
  2.8 0.8 pad_maximum_fusion.own
  3.6 137.1 %sweep.4 = (f32[896,256]{1,0:T(8,128)}, bf16[896,256]{1,0:T(8,128)(2,1)}) custom-call(bf16[8192,7168]{1,0:T(8,128)(2,1)} %data.9, bf16[896,256]{1,0:T(8,128)(2,1)} %pad_maximum_fusion.own), custom_call_target="tpu_custom_call" | custom-call | flops 60129542144 | bytes 234881024 | tf_op jit(solution)/shard_map/sweep/pallas_call | solution.py:470
  140.7 134.5 %sweep.5 = (f32[896,256]{1,0:T(8,128)}, bf16[896,256]{1,0:T(8,128)(2,1)}) custom-call(bf16[8192,7168]{1,0:T(8,128)(2,1)} %data.9, bf16[896,256]{1,0:T(8,128)(2,1)} %get-tuple-element.8.own), custom_call_target="tpu_custom_call" | custom-call | flops 60129542144 | bytes 234881024 | tf_op jit(solution)/shard_map/sweep/pallas_call | solution.py:470
  275.3 134.4 %sweep.6 = (f32[896,256]{1,0:T(8,128)}, bf16[896,256]{1,0:T(8,128)(2,1)}) custom-call(bf16[8192,7168]{1,0:T(8,128)(2,1)} %data.9, bf16[896,256]{1,0:T(8,128)(2,1)} %get-tuple-element.9.own), custom_call_target="tpu_custom_call" | custom-call | flops 60129542144 | bytes 234881024 | tf_op jit(solution)/shard_map/sweep/pallas_call | solution.py:470
  409.7 134.4 %sweep.7 = (f32[896,256]{1,0:T(8,128)}, bf16[896,256]{1,0:T(8,128)(2,1)}) custom-call(bf16[8192,7168]{1,0:T(8,128)(2,1)} %data.9, bf16[896,256]{1,0:T(8,128)(2,1)} %get-tuple-element.10.own), custom_call_target="tpu_custom_call" | custom-call | flops 60129542144 | bytes 234881024 | tf_op jit(solution)/shard_map/sweep/pallas_call | solution.py:470
  544.1 58.7 %ritz.1 = (f32[7168,256]{1,0:T(8,128)}, f32[1,256]{1,0:T(1,128)}) custom-call(bf16[8192,7168]{1,0:T(8,128)(2,1)} %data.9, f32[896,256]{1,0:T(8,128)} %get-tuple-element.11.own), custom_call_target="tpu_custom_call" | custom-call | flops 30064771072 | bytes 117440512 | tf_op jit(solution)/shard_map/ritz/pallas_call | solution.py:504
  602.8 0.0 copy-start
  602.8 6.6 %copy.6 = f32[7168,256]{1,0:T(8,128)} copy(f32[7168,256]{1,0:T(8,128)} %get-tuple-element.16) | data formatting | bytes 14680064
  609.4 0.0 copy-done
  609.4 0.6 copy.7
Async XLA Ops:
  602.8 6.6 %copy-start = (f32[1,256]{1,0:T(1,128)S(1)}, f32[1,256]{1,0:T(1,128)}, u32[]{:S(2)}) copy-start(f32[1,256]{1,0:T(1,128)} %get-tuple-element.13) | copy-start | bytes 3076

commit v6 on v5

--- a/solution.py
+++ b/solution.py
@@ -230,18 +230,22 @@
     by_width(sub, act)
 
 
-def first_pass(place, data, own, landing, basis, ring, acc, ring_sem, gather_sem, second, clear, finish, after):
-    turns = TURNS
-    tile_rows = ring.shape[1]
+def open_ring(place, data, ring, ring_sem):
     for turn in range(DEPTH):
         tile_copy(place, data, ring, ring_sem, turn, turn, first_order, True)
 
+
+def meet(place):
     barrier = pltpu.get_barrier_semaphore()
     for offset in range(1, 8):
         other = lax.rem(place.row * 4 + place.col + offset, 8)
         pl.semaphore_signal(barrier, inc=1, device_id=(0, other // 4, lax.rem(other, 4)), device_id_type=MESH)
     pl.semaphore_wait(barrier, PEERS)
 
+
+def first_pass(place, data, own, landing, basis, ring, acc, ring_sem, gather_sem, second, clear, finish, after):
+    turns = TURNS
+    tile_rows = ring.shape[1]
     piece = (pl.ds(0, place.widths[0] // 2), pl.ds(place.widths[0] // 2, place.widths[1] // 2))
 
     def hand(index, flip_x, flip_y, sub, device):
@@ -325,99 +329,109 @@
         copy.wait_send()
 
 
-def sweep_kernel(data, own, q_ref, low_ref, turned, gram_part, gram_slots, gram, work, inv_low, sum_send, sum_recv, out_send, out_recv, basis, ring, acc, proj_t, part0, part1, twin0, twin1, far0, far1, side0, side1, ring_sem, gather_sem, twin_sem, far_sem, side_sem):
+def sweep_kernel(data, own, q_ref, low, turned, gram_part, gram_slots, gram, work, inv_low, sum_send, sum_recv, out_send, out_recv, basis, ring, acc, proj_t, part0, part1, twin0, twin1, far0, far1, side0, side1, ring_sem, gather_sem, twin_sem, far_sem, side_sem):
     place = Place(data.shape[1])
-    twin, x_side, y_side = place.twin, place.x_side, place.y_side
-    part, from_twin, from_far, from_side = (part0, part1), (twin0, twin1), (far0, far1), (side0, side1)
-    halves = tuple(width // 2 for width in place.widths)
-    width = turned.shape[0]
-    top = width // 2
-    turns = TURNS
-
-    def clear():
-        part0[...] = jnp.zeros_like(part0)
-        part1[...] = jnp.zeros_like(part1)
-
-    def finish(tile, rows):
-        proj_t[tile] = rows.astype(jnp.bfloat16).T
-
-    first_pass(place, data, own, basis, basis, ring, acc, ring_sem, gather_sem, second_order, clear, finish, lambda: None)
-
-    upper, lower = pl.ds(0, top), pl.ds(top, width - top)
-    mine = tuple(pl.ds(pl.multiple_of(place.core * half, HALF), half) for half in halves)
-    other = tuple(pl.ds(pl.multiple_of((1 - place.core) * half, HALF), half) for half in halves)
-    FAR, Y, X, OWN = 0, 1, 2, 3
-
-    def remote(source, target, sems, device):
-        return pltpu.make_async_remote_copy(src_ref=source, dst_ref=target, send_sem=sems.at[0], recv_sem=sems.at[1], device_id=device, device_id_type=MESH)
-
-    swaps, relays, delivers = {}, {}, {}
-    for sub in range(2):
-        for kind in range(4):
-            swaps[kind, sub] = remote(part[sub].at[kind, :, other[sub]], from_twin[sub].at[kind], twin_sem.at[kind, sub], twin)
-        relays[0, sub] = remote(part[sub].at[FAR, upper, mine[sub]], from_far[sub].at[0], far_sem.at[0, sub], x_side)
-        relays[1, sub] = remote(part[sub].at[FAR, lower, mine[sub]], from_far[sub].at[1], far_sem.at[1, sub], y_side)
-        for kind, device in ((Y, y_side), (X, x_side)):
-            for which, rows in ((0, upper), (1, lower)):
-                delivers[kind, which, sub] = remote(part[sub].at[kind, rows, mine[sub]], from_side[sub].at[kind - 1, rows], side_sem.at[kind - 1, which, sub], device)
-
-    def lift(kind, sub):
-        swaps[kind, sub].wait_recv()
-        part[sub][kind, :, mine[sub]] = part[sub][kind, :, mine[sub]] + from_twin[sub][kind]
-
-    def send_far(sub):
-        lift(FAR, sub)
-        relays[0, sub].start()
-        relays[1, sub].start()
-
-    def send_side(kind, sub):
-        lift(kind, sub)
-        plain, joined, rows = (1, 0, upper) if kind == Y else (0, 1, lower)
-        delivers[kind, plain, sub].start()
-        relays[joined, sub].wait_recv()
-        part[sub][kind, rows, mine[sub]] = part[sub][kind, rows, mine[sub]] + from_far[sub][joined]
-        delivers[kind, joined, sub].start()
-
-    order = ((FAR, 0), (FAR, 1), (Y, 0), (X, 0), (Y, 1), (X, 1), (OWN, 0), (OWN, 1))
-
-    @pl.loop(0, turns)
-    def _(turn):
-        slot = lax.rem(turn + turns - TILES, DEPTH)
-        block, tile = turn // TILES, lax.rem(turn, TILES)
-        sub = second_order(block)[2]
-
-        @pl.when(turn >= TILES)
-        def _():
-            tile_copy(place, data, ring, ring_sem, turn, slot, second_order, False)
-
-        kind = jnp.where(block < 2, FAR, jnp.where(block >= 6, OWN, jnp.where((block == 2) | (block == 4), Y, X)))
-
-        def pull(static):
-            part[static][kind] += jnp.dot(proj_t[tile], ring[slot, :, pl.ds(0, place.widths[static])], preferred_element_type=jnp.float32)
-
-        by_width(sub, pull)
-
-        @pl.when(turn + DEPTH < turns)
-        def _():
-            tile_copy(place, data, ring, ring_sem, turn + DEPTH, slot, second_order, True)
-
-        for index, (held, held_sub) in enumerate(order):
-            pl.when(turn == (index + 1) * TILES - 1)(lambda held=held, held_sub=held_sub: swaps[held, held_sub].start())
-            if held == FAR:
-                pl.when(turn == (index + 1) * TILES + 0)(lambda held_sub=held_sub: send_far(held_sub))
-            elif held != OWN:
-                pl.when(turn == (index + 1) * TILES + 0)(lambda held=held, held_sub=held_sub: send_side(held, held_sub))
-
-    for sub in range(2):
-        lanes = pl.ds(sub * halves[0], halves[sub])
-        lift(OWN, sub)
-        for kind in (Y, X):
-            for which in range(2):
-                delivers[kind, which, sub].wait_recv()
-        turned[:, lanes] = (part[sub][OWN, :, mine[sub]] + from_side[sub][0]) + from_side[sub][1]
-    orthonormalize(q_ref, low_ref, turned, gram_part, gram_slots, gram, work, inv_low, sum_send, sum_recv, out_send, out_recv)
-    for copy in (*swaps.values(), *relays.values(), *delivers.values()):
-        copy.wait_send()
+    open_ring(place, data, ring, ring_sem)
+    low[...] = own[...]
+    meet(place)
+
+    @pl.loop(0, SWEEPS)
+    def _(sweep_index):
+        twin, x_side, y_side = place.twin, place.x_side, place.y_side
+        part, from_twin, from_far, from_side = (part0, part1), (twin0, twin1), (far0, far1), (side0, side1)
+        halves = tuple(width // 2 for width in place.widths)
+        width = turned.shape[0]
+        top = width // 2
+        turns = TURNS
+
+        def clear():
+            part0[...] = jnp.zeros_like(part0)
+            part1[...] = jnp.zeros_like(part1)
+
+        def finish(tile, rows):
+            proj_t[tile] = rows.astype(jnp.bfloat16).T
+
+        first_pass(place, data, low, basis, basis, ring, acc, ring_sem, gather_sem, second_order, clear, finish, lambda: None)
+
+        upper, lower = pl.ds(0, top), pl.ds(top, width - top)
+        mine = tuple(pl.ds(pl.multiple_of(place.core * half, HALF), half) for half in halves)
+        other = tuple(pl.ds(pl.multiple_of((1 - place.core) * half, HALF), half) for half in halves)
+        FAR, Y, X, OWN = 0, 1, 2, 3
+
+        def remote(source, target, sems, device):
+            return pltpu.make_async_remote_copy(src_ref=source, dst_ref=target, send_sem=sems.at[0], recv_sem=sems.at[1], device_id=device, device_id_type=MESH)
+
+        swaps, relays, delivers = {}, {}, {}
+        for sub in range(2):
+            for kind in range(4):
+                swaps[kind, sub] = remote(part[sub].at[kind, :, other[sub]], from_twin[sub].at[kind], twin_sem.at[kind, sub], twin)
+            relays[0, sub] = remote(part[sub].at[FAR, upper, mine[sub]], from_far[sub].at[0], far_sem.at[0, sub], x_side)
+            relays[1, sub] = remote(part[sub].at[FAR, lower, mine[sub]], from_far[sub].at[1], far_sem.at[1, sub], y_side)
+            for kind, device in ((Y, y_side), (X, x_side)):
+                for which, rows in ((0, upper), (1, lower)):
+                    delivers[kind, which, sub] = remote(part[sub].at[kind, rows, mine[sub]], from_side[sub].at[kind - 1, rows], side_sem.at[kind - 1, which, sub], device)
+
+        def lift(kind, sub):
+            swaps[kind, sub].wait_recv()
+            part[sub][kind, :, mine[sub]] = part[sub][kind, :, mine[sub]] + from_twin[sub][kind]
+
+        def send_far(sub):
+            lift(FAR, sub)
+            relays[0, sub].start()
+            relays[1, sub].start()
+
+        def send_side(kind, sub):
+            lift(kind, sub)
+            plain, joined, rows = (1, 0, upper) if kind == Y else (0, 1, lower)
+            delivers[kind, plain, sub].start()
+            relays[joined, sub].wait_recv()
+            part[sub][kind, rows, mine[sub]] = part[sub][kind, rows, mine[sub]] + from_far[sub][joined]
+            delivers[kind, joined, sub].start()
+
+        order = ((FAR, 0), (FAR, 1), (Y, 0), (X, 0), (Y, 1), (X, 1), (OWN, 0), (OWN, 1))
+
+        @pl.loop(0, turns)
+        def _(turn):
+            slot = lax.rem(turn + turns - TILES, DEPTH)
+            block, tile = turn // TILES, lax.rem(turn, TILES)
+            sub = second_order(block)[2]
+
+            @pl.when(turn >= TILES)
+            def _():
+                tile_copy(place, data, ring, ring_sem, turn, slot, second_order, False)
+
+            kind = jnp.where(block < 2, FAR, jnp.where(block >= 6, OWN, jnp.where((block == 2) | (block == 4), Y, X)))
+
+            def pull(static):
+                part[static][kind] += jnp.dot(proj_t[tile], ring[slot, :, pl.ds(0, place.widths[static])], preferred_element_type=jnp.float32)
+
+            by_width(sub, pull)
+
+            @pl.when(turn + DEPTH < turns)
+            def _():
+                tile_copy(place, data, ring, ring_sem, turn + DEPTH, slot, second_order, True)
+
+            for index, (held, held_sub) in enumerate(order):
+                pl.when(turn == (index + 1) * TILES - 1)(lambda held=held, held_sub=held_sub: swaps[held, held_sub].start())
+                if held == FAR:
+                    pl.when(turn == (index + 1) * TILES + 0)(lambda held_sub=held_sub: send_far(held_sub))
+                elif held != OWN:
+                    pl.when(turn == (index + 1) * TILES + 0)(lambda held=held, held_sub=held_sub: send_side(held, held_sub))
+
+        for sub in range(2):
+            lanes = pl.ds(sub * halves[0], halves[sub])
+            lift(OWN, sub)
+            for kind in (Y, X):
+                for which in range(2):
+                    delivers[kind, which, sub].wait_recv()
+            turned[:, lanes] = (part[sub][OWN, :, mine[sub]] + from_side[sub][0]) + from_side[sub][1]
+        @pl.when(sweep_index < SWEEPS - 1)
+        def _():
+            open_ring(place, data, ring, ring_sem)
+
+        orthonormalize(q_ref, low, turned, gram_part, gram_slots, gram, work, inv_low, sum_send, sum_recv, out_send, out_recv)
+        for copy in (*swaps.values(), *relays.values(), *delivers.values()):
+            copy.wait_send()
 
 
 def ritz_kernel(data, own, q_ref, r_ref, basis, ring, acc, slots, ring_sem, gather_sem, share_sem):
@@ -448,6 +462,8 @@
             total = total + slots[index]
         r_ref[...] = jnp.sum(total, axis=0, keepdims=True)
 
+    open_ring(place, data, ring, ring_sem)
+    meet(place)
     first_pass(place, data, own, q_ref, basis, ring, acc, ring_sem, gather_sem, None, clear, finish, after)
 
 
@@ -459,7 +475,7 @@
     ]
 
 
-def sweep(data_local, own):
+def sweeps(data_local, own):
     rows, features = data_local.shape
     width = own.shape[1]
     widths = cut_of(features // 4)
@@ -469,10 +485,11 @@
         pairs += [pltpu.VMEM((*shape, size // scale), jnp.float32) for size in widths]
     return pl.pallas_call(
         sweep_kernel,
-        out_shape=(jax.ShapeDtypeStruct((features // 8, width), jnp.float32), jax.ShapeDtypeStruct((features // 8, width), jnp.bfloat16)),
+        out_shape=jax.ShapeDtypeStruct((features // 8, width), jnp.float32),
         in_specs=[pl.BlockSpec(memory_space=pl.ANY), pl.BlockSpec(memory_space=pltpu.VMEM)],
-        out_specs=(pl.BlockSpec(memory_space=pltpu.VMEM), pl.BlockSpec(memory_space=pltpu.VMEM)),
+        out_specs=pl.BlockSpec(memory_space=pltpu.VMEM),
         scratch_shapes=[
+            pltpu.VMEM((features // 8, width), jnp.bfloat16),
             pltpu.VMEM((width, features // 8), jnp.float32),
             pltpu.VMEM((2, 3 * HALF, HALF), jnp.float32),
             pltpu.VMEM((2, PEERS, 3 * HALF // 8, HALF), jnp.float32),
@@ -493,8 +510,8 @@
             pltpu.SemaphoreType.DMA((2, 2, 2, 2)),
         ],
         compiler_params=pltpu.CompilerParams(collective_id=1, has_side_effects=True, vmem_limit_bytes=VMEM_BYTES),
-        cost_estimate=pl.CostEstimate(flops=4 * rows * features * width, bytes_accessed=4 * rows * features, transcendentals=0),
-        name="sweep",
+        cost_estimate=pl.CostEstimate(flops=16 * rows * features * width, bytes_accessed=16 * rows * features, transcendentals=0),
+        name="sweeps",
     )(data_local, own)
 
 
@@ -527,9 +544,7 @@
         base, core = (row * 2 + col // 2) * chip_cols, col % 2
         pieces = (lax.dynamic_slice_in_dim(start_block, base + core * (first // 2), first // 2), lax.dynamic_slice_in_dim(start_block, base + first + core * (second // 2), second // 2))
         low_rows = jnp.concatenate(pieces).astype(jnp.bfloat16)
-        for _ in range(SWEEPS):
-            q_rows, low_rows = sweep(data_local, low_rows)
-        q_basis, ritz_vals = ritz(data_local, q_rows)
+        q_basis, ritz_vals = ritz(data_local, sweeps(data_local, low_rows))
         return q_basis, ritz_vals.reshape(-1)
 
     return jax.shard_map(device_sweeps, mesh=mesh, in_specs=(P(("batch", "row", "col"), None), P("batch", None)), out_specs=(P("batch", None), P("batch")), check_vma=False)

time: 618 us -> 595 us (0.963); the launches traced: 611 us -> 594 us
  Pallas kernels: 599 us -> 584 us
    pallas_call x4 -> x1, Pallas kernels: 541 us -> 525 us  [sweeps(): pl.pallas_call(sweep_kernel, out_shape=jax.ShapeDtypeStruct((features //...]
where the time goes in v6:
time: 595 us; the launch traced here: 594 us
  Pallas kernels  584 us (98%)
  local copies, waits for them, and re-layouts  9.27 us (2%)
    pallas_call x1, Pallas kernels, sweeps(): pl.pallas_call(sweep_kernel, out_shape=jax.ShapeDtypeStruct((features //...  525 us
    pallas_call x1, Pallas kernels, ritz(): pl.pallas_call(ritz_kernel, out_shape=(jax.ShapeDtypeStruct((features, wi...  58.7 us

profile of v6, /device:TPU:0, one launch (start us, length us, event | category | flops | bytes accessed | tf_op | source)
XLA Modules:
  0.0 594.3 jit_solution(17297986894351889582)
XLA Ops:
  0.7 1.0 dynamic-slice_convert_fusion.1
  1.7 1.1 dynamic-slice_convert_fusion
  2.8 0.8 pad_maximum_fusion.own
  3.6 524.8 %sweeps.1.own = f32[896,256]{1,0:T(8,128)} custom-call(bf16[8192,7168]{1,0:T(8,128)(2,1)} %data.3, bf16[896,256]{1,0:T(8,128)(2,1)} %pad_maximum_fusion.own), custom_call_target="tpu_custom_call" | custom-call | flops 240518168576 | bytes 939524096 | tf_op jit(solution)/shard_map/sweeps/pallas_call | solution.py:486
  528.3 58.7 %ritz.1 = (f32[7168,256]{1,0:T(8,128)}, f32[1,256]{1,0:T(1,128)}) custom-call(bf16[8192,7168]{1,0:T(8,128)(2,1)} %data.3, f32[896,256]{1,0:T(8,128)} %sweeps.1.own), custom_call_target="tpu_custom_call" | custom-call | flops 30064771072 | bytes 117440512 | tf_op jit(solution)/shard_map/ritz/pallas_call | solution.py:521
  587.1 0.0 copy-start
  587.1 6.6 %copy.6 = f32[7168,256]{1,0:T(8,128)} copy(f32[7168,256]{1,0:T(8,128)} %get-tuple-element.8) | data formatting | bytes 14680064
  593.7 0.0 copy-done
  593.7 0.6 copy.7
Async XLA Ops:
  587.1 6.6 %copy-start = (f32[1,256]{1,0:T(1,128)S(1)}, f32[1,256]{1,0:T(1,128)}, u32[]{:S(2)}) copy-start(f32[1,256]{1,0:T(1,128)} %get-tuple-element.5) | copy-start | bytes 3076
